TPU v7x, 32 devices: a 4x4x1 block of a 4x4x8 slice. The times are simulated.
32 devices in a mesh: rep: 1 (over z), dp: 32 (over x, y, core).
Axes of the slice: x: 4, y: 4, z: 1, core: 2. Of those that a mesh axis runs over, the one named last changes fastest.
The devices are a block of a 4x4x8 slice.
Arguments:
- x: bfloat16 [32, 2048, 768], P(('rep', 'dp'))
- dy: bfloat16 [32, 2048, 768], P(('rep', 'dp'))
- w_gate: bfloat16 [2, 768, 2304], replicated
- w_up: bfloat16 [2, 768, 2304], replicated
- w_down: bfloat16 [2, 2304, 768], replicated
- m_w_gate: float32 [2, 768, 2304], replicated
- m_w_up: float32 [2, 768, 2304], replicated
- m_w_down: float32 [2, 2304, 768], replicated
- v_w_gate: float32 [2, 768, 2304], replicated
- v_w_up: float32 [2, 768, 2304], replicated
- v_w_down: float32 [2, 2304, 768], replicated
Outputs:
- output 1: bfloat16 [2, 768, 2304], P('rep')
- output 2: bfloat16 [2, 768, 2304], P('rep')
- output 3: bfloat16 [2, 2304, 768], P('rep')
- output 4: float32 [2, 768, 2304], P('rep')
- output 5: float32 [2, 768, 2304], P('rep')
- output 6: float32 [2, 2304, 768], P('rep')
- output 7: float32 [2, 768, 2304], P('rep')
- output 8: float32 [2, 768, 2304], P('rep')
- output 9: float32 [2, 2304, 768], P('rep')
All inputs are finite; a program needn't handle non-finite values.
Results may differ from a plain program's by a relative error of at most 0.022.
Values are sent between devices in bfloat16 or wider.
A program may use at most 768 MiB of HBM per device.

v0:
```python
import jax
import jax.numpy as jnp
from jax import lax
from jax.sharding import PartitionSpec as P

NAMES = ("w_gate", "w_up", "w_down")


def matmul(a, w):
    return jnp.dot(a, w, preferred_element_type=jnp.float32).astype(jnp.bfloat16)


def normed(h):
    wide = h.astype(jnp.float32)
    scale = lax.rsqrt(jnp.mean(wide**2, -1, keepdims=True) + 1e-6)
    return (wide * scale).astype(jnp.bfloat16)


def layer(h, w):
    a = normed(h)
    gate = jnp.dot(a, w["w_gate"], preferred_element_type=jnp.float32)
    up = jnp.dot(a, w["w_up"], preferred_element_type=jnp.float32)
    return h + matmul((jax.nn.silu(gate) * up).astype(jnp.bfloat16), w["w_down"])


def adamw(w, m, v, g):
    m = 0.9 * m + 0.1 * g
    v = 0.95 * v + 0.05 * g * g
    step = m * lax.rsqrt(v + 1e-8) + 0.1 * w
    return (w - 0.02 * step).astype(jnp.bfloat16), m, v


def clipped(gradients, sum_of_squares, count):
    factor = jnp.minimum(1.0, 0.5 * lax.rsqrt(sum_of_squares / count + 1e-30))
    return [g * factor for g in gradients]


def solution(mesh):
    def step(x, dy, *arrays):
        weights, m, v = (arrays[i : i + 3] for i in (0, 3, 6))
        layers = weights[0].shape[0]
        h, kept = x[0], []
        for number in range(layers):
            kept.append(h)
            h = layer(h, {name: w[number] for name, w in zip(NAMES, weights, strict=True)})
        by_h, summed = dy[0], [None] * layers
        for number in reversed(range(layers)):
            _, back = jax.vjp(lambda w, h: layer(h, w), {name: w[number] for name, w in zip(NAMES, weights, strict=True)}, kept[number])
            by_w, by_h = back(by_h)
            summed[number] = [lax.psum(by_w[name], "dp") for name in NAMES]
        gradients = [jnp.stack([summed[number][i] for number in range(layers)]).astype(jnp.float32) for i in range(3)]
        gradients = clipped(gradients, sum(jnp.sum(g * g) for g in gradients), sum(g.size for g in gradients))
        new = [adamw(w.astype(jnp.float32), m, v, g) for w, m, v, g in zip(weights, m, v, gradients, strict=True)]
        return tuple(one[which] for which in range(3) for one in new)

    return jax.shard_map(
        step,
        mesh=mesh,
        in_specs=(P(("rep", "dp"), None, None),) * 2 + (P(None, None, None),) * 9,
        out_specs=(P("rep", None, None),) * 9,
        check_vma=False,
    )
```

profile of v0, /device:TPU:97, one launch (start us, length us, event | category | flops | bytes accessed | tf_op | source)
XLA Modules:
  0.0 538.7 jit_solution(16280703763479636389)
XLA Ops:
  7.2 0.1 all-reduce.3.cloned.1.call-start
  7.3 3.2 copy.20
  10.5 0.0 copy-start.2
  10.5 0.7 fusion.36
  11.2 5.0 copy.21
  16.2 12.5 %convolution_convert_fusion.1 = bf16[2048,2304]{1,0:T(8,128)(2,1)} fusion(bf16[2,2304,768]{2,1,0:T(8,128)(2,1)} %param.15, bf16[1,2048,768]{2,1,0:T(8,128)(2,1)} %param.12), kind=kOutput, calls=%fused_computation.59 | convolution fusion | flops 7252475904 | bytes 16121856 | tf_op jit(solution)/shard_map/transpose(jvp())/dot_general | solution.py:10
  28.7 0.0 copy-done.5
  28.7 13.0 %fusion.70 = f32[2048,2304]{1,0:T(8,128)} fusion(bf16[2,768,2304]{2,1,0:T(8,128)(2,1)} %param.13, bf16[1,2048,768]{2,1,0:T(8,128)(2,1)S(1)} %copy-done.5, f32[2048]{0:T(1024)S(1)} %add_rsqrt_fusion), kind=kOutput, calls=%fused_computation.105 | convolution fusion | flops 7252475904 | bytes 25567232 | tf_op jit(solution)/shard_map/dot_general | solution.py:21
  41.7 0.0 copy-done.11
  41.7 19.0 %multiply_convert_fusion.1 = (bf16[2048,2304]{1,0:T(8,128)(2,1)}, f32[2048,2304]{1,0:T(8,128)}) fusion(f32[2048,2304]{1,0:T(8,128)} %fusion.70, bf16[2,768,2304]{2,1,0:T(8,128)(2,1)} %param.14, bf16[1,2048,768]{2,1,0:T(8,128)(2,1)} %param.11, f32[2048]{0:T(1024)S(1)} %add_rsqrt_fusion), kind=kOutput, calls=%fused_computation.20 | convolution fusion | flops 7280787456 | bytes 53878784 | tf_op jit(solution)/shard_map/dot_general | solution.py:22
  60.7 0.0 copy-done.2
  60.7 11.9 %fusion.40 = (f32[2048]{0:T(1024)S(1)}, bf16[2048,768]{0,1:T(8,128)(2,1)S(1)}) fusion(bf16[2048,2304]{1,0:T(8,128)(2,1)} %get-tuple-element.24, bf16[2,2304,768]{2,1,0:T(8,128)(2,1)} %param.15, bf16[1,2048,768]{1,2,0:T(8,128)(2,1)S(1)} %copy.20), kind=kOutput, calls=%fused_computation.76 | convolution fusion | flops 7255619584 | bytes 19275776 | tf_op jit(solution)/shard_map/dot_general | solution.py:10
  72.5 0.0 copy-start.9
  72.6 0.0 copy-start.7
  72.6 0.6 copy-done.9
  73.1 1.1 copy-done.7
  74.2 13.5 %fusion.57 = f32[2048,2304]{1,0:T(8,128)} fusion(bf16[2,768,2304]{2,1,0:T(8,128)(2,1)} %param.14, bf16[2048,768]{0,1:T(8,128)(2,1)S(1)} %get-tuple-element.27, f32[2048]{0:T(1024)S(1)} %fusion.108), kind=kOutput, calls=%fused_computation.92 | convolution fusion | flops 7252475904 | bytes 25567232 | tf_op jit(solution)/shard_map/jvp()/dot_general | solution.py:22
  87.8 30.5 %fusion.2 = (bf16[2048,2304]{1,0:T(8,128)(2,1)}, f32[2048,2304]{1,0:T(8,128)}) fusion(f32[2048,2304]{1,0:T(8,128)} %fusion.57, bf16[2048,2304]{1,0:T(8,128)(2,1)} %convolution_convert_fusion.1, bf16[2,768,2304]{2,1,0:T(8,128)(2,1)} %param.13, bf16[2048,768]{0,1:T(8,128)(2,1)} %copy-done.7, f32[2048]{0:T(1024)S(1)} %fusion.108), kind=kOutput, calls=%fused_computation.11 | convolution fusion | flops 7309099008 | bytes 63315968 | tf_op jit(solution)/shard_map/jvp()/dot_general | solution.py:21
  118.3 0.0 slice-done.2
  118.3 0.0 slice-done.3
  118.3 0.0 copy-start.8
  118.3 0.0 copy-start.13
  118.3 11.3 %fusion.78 = bf16[2048,768]{0,1:T(8,128)(2,1)} fusion(bf16[2048,2304]{1,0:T(8,128)(2,1)} %get-tuple-element.28, bf16[2,768,2304]{2,1,0:T(8,128)(2,1)S(1)} %bitcast.83), kind=kOutput, calls=%fused_computation.111 | convolution fusion | flops 7247757312 | bytes 16121856 | tf_op jit(solution)/shard_map/transpose(jvp())/dot_general | solution.py:21
  129.7 0.0 copy-done.8
  129.7 0.0 copy-done.13
  129.7 8.9 %fusion.50 = bf16[1,768,2304]{2,1,0:T(8,128)(2,1)} fusion(bf16[2048,2304]{1,0:T(8,128)(2,1)S(1)} %copy-done.13, bf16[2048,768]{0,1:T(8,128)(2,1)S(1)} %copy-done.8, f32[2048]{0:T(1024)S(1)} %fusion.108), kind=kOutput, calls=%fused_computation.87 | convolution fusion | flops 7252475904 | bytes 16130048 | tf_op jit(solution)/shard_map/transpose(jvp())/dot_general | solution.py:21
  138.6 0.0 copy-done.6
  138.6 18.0 %fusion.49 = bf16[1,2304,768]{2,1,0:T(8,128)(2,1)} fusion(f32[2048,2304]{1,0:T(8,128)} %fusion.57, bf16[1,2048,768]{2,1,0:T(8,128)(2,1)S(1)} %copy-done.6, f32[2048,2304]{1,0:T(8,128)} %get-tuple-element.29), kind=kOutput, calls=%fused_computation.86 | convolution fusion | flops 7277838336 | bytes 44433408 | tf_op jit(solution)/shard_map/transpose(jvp())/dot_general | solution.py:10
  156.6 16.4 %fusion.56 = bf16[1,768,2304]{2,1,0:T(8,128)(2,1)} fusion(bf16[2048,2304]{1,0:T(8,128)(2,1)} %convolution_convert_fusion.1, bf16[2048,768]{0,1:T(8,128)(2,1)} %copy-done.7, f32[2048]{0:T(1024)S(1)} %fusion.108, f32[2048,2304]{1,0:T(8,128)} %get-tuple-element.29), kind=kOutput, calls=%fused_computation.91 | convolution fusion | flops 7282556928 | bytes 35004416 | tf_op jit(solution)/shard_map/transpose(jvp())/dot_general | solution.py:22
  173.0 19.6 %fusion.42 = (f32[2048]{0:T(1024)S(1)}, bf16[2048,768]{0,1:T(8,128)(2,1)}) fusion(bf16[2048,768]{0,1:T(8,128)(2,1)} %copy-done.7, bf16[2048,768]{0,1:T(8,128)(2,1)} %fusion.78, bf16[2,768,2304]{2,1,0:T(8,128)(2,1)} %param.14, bf16[2048,2304]{1,0:T(8,128)(2,1)} %convolution_convert_fusion.1, f32[2048,2304]{1,0:T(8,128)} %get-tuple-element.29), kind=kOutput, calls=%fused_computation.78 | convolution fusion | flops 7285504000 | bytes 41295872 | tf_op jit(solution)/shard_map/transpose(jvp())/dot_general | solution.py:22
  192.6 0.0 copy-done.10
  192.6 0.0 copy-done.4
  192.6 0.0 slice-start
  192.6 5.2 fusion.86
  197.8 0.0 slice-start.1
  197.8 11.6 %fusion.51 = bf16[1,2304,768]{2,1,0:T(8,128)(2,1)} fusion(bf16[2048,2304]{1,0:T(8,128)(2,1)} %get-tuple-element.24, bf16[2048,768]{0,1:T(8,128)(2,1)S(1)} %fusion.86), kind=kOutput, calls=%fused_computation.88 | convolution fusion | flops 7249526784 | bytes 16121856 | tf_op jit(solution)/shard_map/transpose(jvp())/dot_general | solution.py:10
  209.4 0.0 slice-done
  209.4 0.0 slice-done.1
  209.5 10.2 %convolution_convert_fusion = bf16[2048,2304]{1,0:T(8,128)(2,1)} fusion(bf16[2048,768]{0,1:T(8,128)(2,1)S(1)} %fusion.86, bf16[2,2304,768]{2,1,0:T(8,128)(2,1)S(1)} %bitcast.81), kind=kOutput, calls=%fused_computation.58 | convolution fusion | flops 7252475904 | bytes 16121856 | tf_op jit(solution)/shard_map/transpose(jvp())/dot_general | solution.py:10
  219.7 15.6 %fusion.52 = bf16[1,768,2304]{2,1,0:T(8,128)(2,1)} fusion(bf16[2048,2304]{1,0:T(8,128)(2,1)} %convolution_convert_fusion, f32[2048,2304]{1,0:T(8,128)} %fusion.70, bf16[1,2048,768]{1,2,0:T(8,128)(2,1)S(1)} %copy-done.3, f32[2048]{0:T(1024)S(1)} %copy-done.12), kind=kOutput, calls=%fused_computation.89 | convolution fusion | flops 7282556928 | bytes 35004416 | tf_op jit(solution)/shard_map/transpose(jvp())/dot_general | solution.py:22
  235.3 20.4 %fusion.53 = bf16[1,768,2304]{2,1,0:T(8,128)(2,1)} fusion(f32[2048,2304]{1,0:T(8,128)} %fusion.70, f32[2048,2304]{1,0:T(8,128)} %get-tuple-element.25, bf16[2048,2304]{1,0:T(8,128)(2,1)} %convolution_convert_fusion, bf16[1,2048,768]{1,2,0:T(8,128)(2,1)S(1)} %copy-done.3, f32[2048]{0:T(1024)S(1)} %copy-done.12), kind=kOutput, calls=%fused_computation.90 | convolution fusion | flops 7306149888 | bytes 53878784 | tf_op jit(solution)/shard_map/transpose(jvp())/dot_general | solution.py:21
  255.7 0.1 all-reduce.3.cloned.1.call-update
  255.8 182.3 %all-reduce.3.cloned.1.call-done = (bf16[1,768,2304]{2,1,0:T(8,128)(2,1)}, bf16[1,768,2304]{2,1,0:T(8,128)(2,1)}, bf16[1,768,2304]{2,1,0:T(8,128)(2,1)}, bf16[1,...) async-done(((bf16[1,768,2304]{2,1,0:T(8,128)(2,1)}, bf16[1,768,2304]{2,1,0:T(8,128)(2,1)}, bf16[1,768,2304]{2,1,0:T(8,128)(2,1)}, ...) | async-done | bytes 21233680 | tf_op jit(solution)/shard_map/psum | solution.py:50
  438.0 7.5 %fusion.22 = f32[]{:T(128)} fusion(bf16[1,2304,768]{2,1,0:T(8,128)(2,1)} %get-tuple-element.13, bf16[1,2304,768]{2,1,0:T(8,128)(2,1)} %get-tuple-element.14), kind=kLoop, calls=%fused_computation.46 | loop fusion | flops 14155775 | bytes 7077892 | tf_op jit(solution)/shard_map/reduce_sum | solution.py:52
  445.5 7.3 %fusion.21 = f32[]{:T(128)} fusion(bf16[1,768,2304]{2,1,0:T(8,128)(2,1)} %get-tuple-element.11, bf16[1,768,2304]{2,1,0:T(8,128)(2,1)} %get-tuple-element.12), kind=kLoop, calls=%fused_computation.45 | loop fusion | flops 14155775 | bytes 7077892 | tf_op jit(solution)/shard_map/reduce_sum | solution.py:52
  452.8 4.2 fusion.20
  459.0 24.8 %fusion.28 = (bf16[2,2304,768]{2,1,0:T(8,128)(2,1)}, f32[2,2304,768]{2,1,0:T(8,128)}, f32[2,2304,768]{2,1,0:T(8,128)}) fusion(bf16[2,2304,768]{2,1,0:T(8,128)(2,1)} %param.15, f32[]{:T(128)S(6)} %min_shard_map.3, bf16[1,2304,768]{2,1,0:T(8,128)(2,1)} %get-tuple-element.13, bf16[1,2304,768]{2,1,0:T(8,128)(2,1)} %get-tuple-element.14, ...), kind=kLoop, calls=%fused_computation.52 | loop fusion | flops 70778880 | bytes 77856768 | tf_op jit(solution)/shard_map/convert_element_type | solution.py:30
  483.8 47.5 %fusion.19 = (bf16[2,768,2304]{2,1,0:T(8,128)(2,1)}, f32[2,768,2304]{2,1,0:T(8,128)}, f32[2,768,2304]{2,1,0:T(8,128)}, bf16[2,768,2304]{2,1,0:T(8,128)(2,1)}, f3...) fusion(bf16[2,768,2304]{2,1,0:T(8,128)(2,1)} %param.13, f32[]{:T(128)S(6)} %min_shard_map.3, ...), kind=kLoop, calls=%fused_computation.43 | loop fusion | flops 141557760 | bytes 155713536 | tf_op jit(solution)/shard_map/convert_element_type | solution.py:30
  (20 shorter events, 0.1 us)
Async XLA Ops:
  7.2 430.8 %all-reduce.3.cloned.1.call-start = ((), (), s32[]{:S(2)}) async-start(), calls=%async_computation | async-start | bytes 42467328 | tf_op jit(solution)/shard_map/psum | solution.py:50
  10.5 50.2 %copy-start.2 = (bf16[1,2048,768]{1,2,0:T(8,128)(2,1)}, bf16[1,2048,768]{1,2,0:T(8,128)(2,1)S(1)}, u32[]{:S(2)}) copy-start(bf16[1,2048,768]{1,2,0:T(8,128)(2,1)S(1)} %copy.20) | copy-start | bytes 9437188
  11.1 30.6 %copy-start.11 = (f32[2048]{0:T(1024)}, f32[2048]{0:T(1024)S(1)}, u32[]{:S(2)}) copy-start(f32[2048]{0:T(1024)S(1)} %add_rsqrt_fusion) | copy-start | bytes 24580
  16.2 12.6 %copy-start.5 = (bf16[1,2048,768]{2,1,0:T(8,128)(2,1)S(1)}, bf16[1,2048,768]{2,1,0:T(8,128)(2,1)}, u32[]{:S(2)}) copy-start(bf16[1,2048,768]{2,1,0:T(8,128)(2,1)} %param.11) | copy-start | bytes 9437188
  72.5 0.6 copy-start.9
  72.6 1.7 copy-start.7
  74.2 44.1 %slice-start.2 = ((s8[7077888]{0:T(1024)(128)(4,1)}), s8[4194304]{0:T(1024)(128)(4,1)S(1)}, s32[]{:S(2)}) async-start(s8[7077888]{0:T(1024)(128)(4,1)} %bitcast.82), calls=%async_computation.3 | async-start | bytes 8388608
  87.8 30.5 %slice-start.3 = ((s8[7077888]{0:T(1024)(128)(4,1)}), s8[2883584]{0:T(1024)(128)(4,1)S(1)}, s32[]{:S(2)}) async-start(s8[7077888]{0:T(1024)(128)(4,1)} %bitcast.82), calls=%async_computation.4 | async-start | bytes 5767168
  118.3 11.4 %copy-start.8 = (bf16[2048,768]{0,1:T(8,128)(2,1)S(1)}, bf16[2048,768]{0,1:T(8,128)(2,1)}, u32[]{:S(2)}) copy-start(bf16[2048,768]{0,1:T(8,128)(2,1)} %copy-done.7) | copy-start | bytes 9437188
  118.3 11.3 %copy-start.13 = (bf16[2048,2304]{1,0:T(8,128)(2,1)S(1)}, bf16[2048,2304]{1,0:T(8,128)(2,1)}, u32[]{:S(2)}) copy-start(bf16[2048,2304]{1,0:T(8,128)(2,1)} %get-tuple-element.28) | copy-start | bytes 28311556
  129.7 8.9 %copy-start.6 = (bf16[1,2048,768]{2,1,0:T(8,128)(2,1)S(1)}, bf16[1,2048,768]{2,1,0:T(8,128)(2,1)}, u32[]{:S(2)}) copy-start(bf16[1,2048,768]{2,1,0:T(8,128)(2,1)} %param.12) | copy-start | bytes 9437188
  173.0 19.6 %copy-start.10 = (f32[2048]{0:T(1024)S(1)}, f32[2048]{0:T(1024)}, u32[]{:S(2)}) copy-start(f32[2048]{0:T(1024)} %copy-done.9) | copy-start | bytes 24580
  173.0 19.6 %copy-start.4 = (bf16[1,2048,768]{1,2,0:T(8,128)(2,1)S(1)}, bf16[1,2048,768]{1,2,0:T(8,128)(2,1)}, u32[]{:S(2)}) copy-start(bf16[1,2048,768]{1,2,0:T(8,128)(2,1)} %copy.21) | copy-start | bytes 9437188
  192.6 16.8 %slice-start = ((s8[7077888]{0:T(1024)(128)(4,1)}), s8[4194304]{0:T(1024)(128)(4,1)S(1)}, s32[]{:S(2)}) async-start(s8[7077888]{0:T(1024)(128)(4,1)} %bitcast.80), calls=%async_computation.1 | async-start | bytes 8388608
  197.8 11.6 %slice-start.1 = ((s8[7077888]{0:T(1024)(128)(4,1)}), s8[2883584]{0:T(1024)(128)(4,1)S(1)}, s32[]{:S(2)}) async-start(s8[7077888]{0:T(1024)(128)(4,1)} %bitcast.80), calls=%async_computation.2 | async-start | bytes 5767168
  209.4 10.2 %copy-start.3 = (bf16[1,2048,768]{1,2,0:T(8,128)(2,1)S(1)}, bf16[1,2048,768]{1,2,0:T(8,128)(2,1)}, u32[]{:S(2)}) copy-start(bf16[1,2048,768]{1,2,0:T(8,128)(2,1)} %copy-done.2) | copy-start | bytes 9437188
  209.4 10.2 %copy-start.12 = (f32[2048]{0:T(1024)S(1)}, f32[2048]{0:T(1024)}, u32[]{:S(2)}) copy-start(f32[2048]{0:T(1024)} %copy-done.11) | copy-start | bytes 24580
  438.0 14.8 %copy-start = (bf16[1,768,2304]{2,1,0:T(8,128)(2,1)S(1)}, bf16[1,768,2304]{2,1,0:T(8,128)(2,1)}, u32[]{:S(2)}) copy-start(bf16[1,768,2304]{2,1,0:T(8,128)(2,1)} %get-tuple-element.9) | copy-start | bytes 10616836
  438.0 14.8 %copy-start.1 = (bf16[1,768,2304]{2,1,0:T(8,128)(2,1)S(1)}, bf16[1,768,2304]{2,1,0:T(8,128)(2,1)}, u32[]{:S(2)}) copy-start(bf16[1,768,2304]{2,1,0:T(8,128)(2,1)} %get-tuple-element.10) | copy-start | bytes 10616836
Sparse Core Ops, SparseCore 0:
  255.9 182.0 all-reduce.2
where the time goes:
time: 546 us; the launch traced here: 539 us
  matrix products  232 us (42%)
  waiting for transfers between devices  182 us (33%)
  other arithmetic  97.2 us (18%)
  between operations  16.7 us (3%)
  local copies, waits for them, and re-layouts  9.94 us (2%)
    psum x1, waiting for transfers between devices, step(): summed[number] = [lax.psum(by_w[name], 'dp') for name in NAMES]  182 us
    dot_general x5, matrix products, layer(): gate = jnp.dot(a, w['w_gate'], preferred_element_type=jnp.float32)  84.2 us
    dot_general x5, matrix products, layer(): up = jnp.dot(a, w['w_up'], preferred_element_type=jnp.float32)  84 us
    convert_element_type x2, other arithmetic, adamw(): return ((w - 0.02 * step).astype(jnp.bfloat16), m, v)  72.3 us
    dot_general x5, matrix products, matmul(): jnp.dot(a, w, preferred_element_type=jnp.float32).astype(jnp.bfloat16)  64.2 us
    reduce_sum x3, other arithmetic, step(): jnp.sum(g * g)  19 us
  transfers between devices with their start and end apart: 1, of which 1 were waited for; matrix products, arithmetic and copies ran while one was open for 0% of the time, Pallas kernels for 0%

commit v1 on v0

v1 whole, which is shorter than its diff:
```python
import functools
import jax, jax.numpy as jnp
from jax import lax
from jax.experimental import pallas as pl
from jax.experimental.pallas import tpu as pltpu
from jax.sharding import PartitionSpec as P
F32,BF=jnp.float32,jnp.bfloat16
ANY=pl.BlockSpec(memory_space=pl.ANY)
VM=pl.BlockSpec(memory_space=pltpu.VMEM)
def dot(a,b,dims=((1,),(0,))):
    return lax.dot_general(a,b,(dims,((),())),preferred_element_type=F32)
NT=((1,),(1,)); TN=((0,),(0,))
def norm_scale(wide): return lax.rsqrt(jnp.mean(wide*wide,-1,keepdims=True)+1e-6)
def normed(h):
    wide=h.astype(F32); return (wide*norm_scale(wide)).astype(BF)
def sigmoid(g): return 0.5*jnp.tanh(0.5*g)+0.5

def k1_body(x_ref,wg,wu,wd,gate_ref,up_ref,h_ref,a_ref,act,*,fc):
    x=x_ref[...]; a=normed(x); F=wg.shape[1]
    for c in range(F//fc):
        s=pl.ds(c*fc,fc)
        g=dot(a,wg[:,s]); u=dot(a,wu[:,s])
        gate_ref[:,s]=g; up_ref[:,s]=u
        act[:,s]=(g*sigmoid(g)*u).astype(BF)
    d=dot(act[...],wd[...]).astype(BF)
    h=(x.astype(F32)+d.astype(F32)).astype(BF)
    h_ref[...]=h; a_ref[...]=normed(h)
def k1(x,wg,wu,wd,bm=512,fc=768):
    T,D=x.shape; F=wg.shape[2]
    wspec=lambda r,c:pl.BlockSpec((None,r,c),lambda i:(0,0,0),pipeline_mode=pl.Buffered(1))
    row=lambda c:pl.BlockSpec((bm,c),lambda i:(i,0))
    return pl.pallas_call(functools.partial(k1_body,fc=fc),grid=(T//bm,),
        in_specs=[row(D),wspec(D,F),wspec(D,F),wspec(F,D)],
        out_specs=[row(F),row(F),row(D),row(D)],
        out_shape=[jax.ShapeDtypeStruct((T,F),F32)]*2+[jax.ShapeDtypeStruct((T,D),BF)]*2,
        scratch_shapes=[pltpu.VMEM((bm,F),BF)],
        compiler_params=pltpu.CompilerParams(vmem_limit_bytes=60<<20),name="k1",
        cost_estimate=pl.CostEstimate(flops=6*T*D*F,bytes_accessed=10*T*F,transcendentals=T*F))(x,wg,wu,wd)

def k2_body(a_ref,dy_ref,h_ref,wg_h,wu_h,wd_h,dwg,dwu,dwd,dh_ref,wg,wu,wd,aT,dg,du,act,sem,*,nf,ft,rc,bc):
    j=pl.program_id(0); T,D=a_ref.shape; L=1
    cps=lambda t:[pltpu.make_async_copy(wg_h.at[L,:,pl.ds(t*ft,ft)],wg.at[:,pl.ds(t*ft,ft)],sem.at[0,t]),
                  pltpu.make_async_copy(wu_h.at[L,:,pl.ds(t*ft,ft)],wu.at[:,pl.ds(t*ft,ft)],sem.at[1,t]),
                  pltpu.make_async_copy(wd_h.at[L,pl.ds(t*ft,ft),:],wd.at[pl.ds(t*ft,ft),:],sem.at[2,t])]
    @pl.when(j==0)
    def _():
        for t in range(nf):
            for c in cps(t): c.start()
        for r in range(T//512): aT[:,pl.ds(r*512,512)]=a_ref[pl.ds(r*512,512),:].T
    @pl.when(j<nf)
    def _():
        for c in cps(j): c.wait()
        off=pl.multiple_of(j*ft,ft); s=pl.ds(off,ft)
        wgt,wut,wdt=wg[:,s],wu[:,s],wd[s,:]
        for r in range(T//rc):
            rs=pl.ds(r*rc,rc)
            a=a_ref[rs,:]
            g=dot(a,wgt); u=dot(a,wut); da=dot(dy_ref[rs,:],wdt,NT).astype(BF).astype(F32)
            sg=sigmoid(g); silu=g*sg
            act[rs,:]=(silu*u).astype(BF)
            du[rs,s]=(da*silu).astype(BF)
            dg[rs,s]=(da*u*(sg+silu*(1.0-sg))).astype(BF)
        dwg[...]=dot(aT[...],dg[:,s]).astype(BF)
        dwu[...]=dot(aT[...],du[:,s]).astype(BF)
        dwd[...]=dot(act[...],dy_ref[...],TN).astype(BF)
    @pl.when(j>=nf)
    def _():
        r=pl.multiple_of((j-nf)*bc,bc); rs=pl.ds(r,bc)
        da=(dot(dg[rs,:],wg[...],NT).astype(BF).astype(F32)+dot(du[rs,:],wu[...],NT).astype(BF).astype(F32)).astype(BF).astype(F32)
        wide=h_ref[rs,:].astype(F32); sc=norm_scale(wide)
        t=jnp.sum(da*wide,-1,keepdims=True)*(1.0/D)
        dn=(da*sc-wide*(sc*sc*sc*t)).astype(BF).astype(F32)
        dh_ref[rs,:]=(dy_ref[rs,:].astype(F32)+dn).astype(BF)
def k2(a1,dy,h1,wg,wu,wd,ft=256,rc=512,bc=512):
    T,D=a1.shape; F=wg.shape[2]; nf=F//ft; nb=T//bc
    col=pl.BlockSpec((D,ft),lambda j:(0,jnp.minimum(j,nf-1))); rowb=pl.BlockSpec((ft,D),lambda j:(jnp.minimum(j,nf-1),0))
    return pl.pallas_call(functools.partial(k2_body,nf=nf,ft=ft,rc=rc,bc=bc),grid=(nf+nb,),
        in_specs=[VM,VM,VM,ANY,ANY,ANY],out_specs=[col,col,rowb,pl.BlockSpec((T,D),lambda j:(0,0))],
        out_shape=[jax.ShapeDtypeStruct((D,F),BF)]*2+[jax.ShapeDtypeStruct((F,D),BF),jax.ShapeDtypeStruct((T,D),BF)],
        scratch_shapes=[pltpu.VMEM((D,F),BF),pltpu.VMEM((D,F),BF),pltpu.VMEM((F,D),BF),pltpu.VMEM((D,T),BF),
                        pltpu.VMEM((T,F),BF),pltpu.VMEM((T,F),BF),pltpu.VMEM((T,ft),BF),pltpu.SemaphoreType.DMA((3,nf))],
        compiler_params=pltpu.CompilerParams(vmem_limit_bytes=63<<20),name="k2",
        cost_estimate=pl.CostEstimate(flops=16*T*D*F,bytes_accessed=30<<20,transcendentals=T*F))(a1,dy,h1,wg,wu,wd)

def k3_body(x_ref,dh_ref,g_ref,u_ref,wd_ref,dwg,dwu,dwd,aT,dg,du,act,*,rc):
    j=pl.program_id(0); T,D=x_ref.shape
    @pl.when(j==0)
    def _():
        for r in range(T//512): aT[:,pl.ds(r*512,512)]=normed(x_ref[pl.ds(r*512,512),:]).T
    wdt=wd_ref[...]
    for r in range(T//rc):
        rs=pl.ds(r*rc,rc)
        da=dot(dh_ref[rs,:],wdt,NT).astype(BF).astype(F32)
        g=g_ref[rs,:]; u=u_ref[rs,:]
        sg=sigmoid(g); silu=g*sg
        act[rs,:]=(silu*u).astype(BF)
        du[rs,:]=(da*silu).astype(BF)
        dg[rs,:]=(da*u*(sg+silu*(1.0-sg))).astype(BF)
    dwg[...]=dot(aT[...],dg[...]).astype(BF)
    dwu[...]=dot(aT[...],du[...]).astype(BF)
    dwd[...]=dot(act[...],dh_ref[...],TN).astype(BF)
def k3(x,dh,gate,up,wd,ft=256,rc=512):
    T,D=x.shape; F=gate.shape[1]; nf=F//ft
    col=lambda r:pl.BlockSpec((r,ft),lambda j:(0,j))
    return pl.pallas_call(functools.partial(k3_body,rc=rc),grid=(nf,),
        in_specs=[VM,VM,col(T),col(T),pl.BlockSpec((None,ft,D),lambda j:(0,j,0))],
        out_specs=[col(D),col(D),pl.BlockSpec((ft,D),lambda j:(j,0))],
        out_shape=[jax.ShapeDtypeStruct((D,F),BF)]*2+[jax.ShapeDtypeStruct((F,D),BF)],
        scratch_shapes=[pltpu.VMEM((D,T),BF)]+[pltpu.VMEM((T,ft),BF)]*3,
        compiler_params=pltpu.CompilerParams(vmem_limit_bytes=60<<20),name="k3",
        cost_estimate=pl.CostEstimate(flops=8*T*D*F,bytes_accessed=10*T*F,transcendentals=T*F))(x,dh,gate,up,wd)


def adamw(w, m, v, g):
    m = 0.9 * m + 0.1 * g
    v = 0.95 * v + 0.05 * g * g
    step = m * lax.rsqrt(v + 1e-8) + 0.1 * w
    return (w - 0.02 * step).astype(jnp.bfloat16), m, v


def clipped(gradients, sum_of_squares, count):
    factor = jnp.minimum(1.0, 0.5 * lax.rsqrt(sum_of_squares / count + 1e-30))
    return [g * factor for g in gradients]


def solution(mesh):
    def step(x, dy, *arrays):
        weights, m, v = (arrays[i : i + 3] for i in (0, 3, 6))
        gate, up, h1, a1 = k1(x[0], *weights)
        *of1, dh = k2(a1, dy[0], h1, *weights)
        of0 = k3(x[0], dh, gate, up, weights[2])
        summed = [[lax.psum(g, "dp") for g in one] for one in (of0, of1)]
        gradients = [jnp.stack([one[i] for one in summed]).astype(F32) for i in range(3)]
        gradients = clipped(gradients, sum(jnp.sum(g * g) for g in gradients), sum(g.size for g in gradients))
        new = [adamw(w.astype(F32), m, v, g) for w, m, v, g in zip(weights, m, v, gradients, strict=True)]
        return tuple(one[which] for which in range(3) for one in new)

    return jax.shard_map(
        step,
        mesh=mesh,
        in_specs=(P(("rep", "dp"), None, None),) * 2 + (P(None, None, None),) * 9,
        out_specs=(P("rep", None, None),) * 9,
        check_vma=False,
    )
```

time: 546 us -> 435 us (0.80); the launches traced: 539 us -> 435 us
  matrix products: 232 us -> 0 us
  Pallas kernels: 0 us -> 143 us
  local copies, waits for them, and re-layouts: 9.94 us -> 0.01 us
    dot_general x15 -> x0, matrix products: 232 us -> none  [the longest x5 84.2 us: layer(): gate = jnp.dot(a, w['w_gate'], preferred_element_type=jnp.float32)]
    pallas_call x0 -> x3, Pallas kernels: none -> 143 us  [the longest x1 72.2 us: k2(): pl.pallas_call(functools.partial(k2_body, nf=nf, ft=ft, rc=rc, bc=bc), gr...]
    unnamed x38 -> x4, local copies, waits for them, and re-layouts: 9.94 us -> 0.01 us
where the time goes in v1:
time: 435 us
  waiting for transfers between devices  182 us (42%)
  Pallas kernels  143 us (33%)
  other arithmetic  93.5 us (21%)
  between operations  16.1 us (4%)
    psum x1, waiting for transfers between devices, step(): summed = [[lax.psum(g, 'dp') for g in one] for one in (of0, of1)]  182 us
    convert_element_type x2, other arithmetic, adamw(): return ((w - 0.02 * step).astype(jnp.bfloat16), m, v)  72.4 us
    pallas_call x1, Pallas kernels, k2(): pl.pallas_call(functools.partial(k2_body, nf=nf, ft=ft, rc=rc, bc=bc), gr...  72.2 us
    pallas_call x1, Pallas kernels, k3(): pl.pallas_call(functools.partial(k3_body, rc=rc), grid=(nf,), in_specs=[V...  39.7 us
    pallas_call x1, Pallas kernels, k1(): pl.pallas_call(functools.partial(k1_body, fc=fc), grid=(T // bm,), in_spe...  30.8 us
    reduce_sum x3, other arithmetic, step(): jnp.sum(g * g)  21 us
  transfers between devices with their start and end apart: 1, of which 1 were waited for; matrix products, arithmetic and copies ran while one was open for 0% of the time, Pallas kernels for 0%

profile of v1, /device:TPU:97, one launch (start us, length us, event | category | flops | bytes accessed | tf_op | source)
XLA Modules:
  0.0 434.6 jit_solution(6281052360155741669)
XLA Ops:
  7.2 0.1 all-reduce.3.cloned.1.call-start
  7.3 30.8 %k1.1 = (f32[2048,2304]{1,0:T(8,128)}, f32[2048,2304]{1,0:T(8,128)}, bf16[2048,768]{1,0:T(8,128)(2,1)}, bf16[2048,768]{1,0:T(8,128)(2,1)}) custom-call(bf16[2048,768]{1,0:T(8,128)(2,1)} %bitcast.15, bf16[2,768,2304]{2,1,0:T(8,128)(2,1)} %wg_h.1, bf16[2,768,2304]{2,1,0:T(8,128)(2,1)} %wu_h.1, bf16[2,2304,768]{2,1,0:T(8,128)(2,1)} %wd_ref.1), custom_call_target="tpu_custom_call" | custom-call | flops 21743271936 | bytes 47185920 | tf_op jit(solution)/shard_map/k1/pallas_call | solution.py:32
  38.0 72.2 %k2.1 = (bf16[768,2304]{1,0:T(8,128)(2,1)}, bf16[768,2304]{1,0:T(8,128)(2,1)}, bf16[2304,768]{1,0:T(8,128)(2,1)}, bf16[2048,768]{1,0:T(8,128)(2,1)}) custom-call(bf16[2048,768]{1,0:T(8,128)(2,1)} %get-tuple-element.20.a_ref, bf16[2048,768]{1,0:T(8,128)(2,1)} %bitcast.14, bf16[2048,768]{1,0:T(8,128)(2,1)} %get-tuple-element.21.h_ref, ...), custom_call_target="tpu_custom_call" | custom-call | flops 57982058496 | bytes 31457280 | tf_op jit(solution)/shard_map/k2/pallas_call | solution.py:77
  110.2 39.7 %k3.1 = (bf16[768,2304]{1,0:T(8,128)(2,1)}, bf16[768,2304]{1,0:T(8,128)(2,1)}, bf16[2304,768]{1,0:T(8,128)(2,1)}) custom-call(bf16[2048,768]{1,0:T(8,128)(2,1)} %bitcast.16, bf16[2048,768]{1,0:T(8,128)(2,1)} %get-tuple-element.22.dh_ref, f32[2048,2304]{1,0:T(8,128)} %get-tuple-element.23.g_ref, f32[2048,2304]{1,0:T(8,128)} %get-tuple-element.24.u_ref, ...), custom_call_target="tpu_custom_call" | custom-call | flops 28991029248 | bytes 47185920 | tf_op jit(solution)/shard_map/k3/pallas_call | solution.py:105
  149.9 0.1 all-reduce.3.cloned.1.call-update
  150.0 182.3 %all-reduce.3.cloned.1.call-done = (bf16[1,768,2304]{2,1,0:T(8,128)(2,1)}, bf16[1,768,2304]{2,1,0:T(8,128)(2,1)}, bf16[1,768,2304]{2,1,0:T(8,128)(2,1)}, bf16[1,...) async-done(((bf16[1,768,2304]{2,1,0:T(8,128)(2,1)}, bf16[1,768,2304]{2,1,0:T(8,128)(2,1)}, bf16[1,768,2304]{2,1,0:T(8,128)(2,1)}, ...) | async-done | bytes 21233680 | tf_op jit(solution)/shard_map/psum | solution.py:132
  332.2 0.0 copy-start.1
  332.2 7.5 %fusion.9 = f32[]{:T(128)} fusion(bf16[1,768,2304]{2,1,0:T(8,128)(2,1)} %get-tuple-element.31, bf16[1,768,2304]{2,1,0:T(8,128)(2,1)} %get-tuple-element.32), kind=kLoop, calls=%fused_computation.24 | loop fusion | flops 14155775 | bytes 7077892 | tf_op jit(solution)/shard_map/reduce_sum | solution.py:134
  339.7 7.3 %fusion.10 = f32[]{:T(128)} fusion(bf16[1,768,2304]{2,1,0:T(8,128)(2,1)} %get-tuple-element.33, bf16[1,768,2304]{2,1,0:T(8,128)(2,1)} %get-tuple-element.34), kind=kLoop, calls=%fused_computation.25 | loop fusion | flops 14155775 | bytes 7077892 | tf_op jit(solution)/shard_map/reduce_sum | solution.py:134
  348.3 0.0 copy-done.1
  348.3 6.2 %fusion.11 = f32[]{:T(128)} fusion(bf16[1,2304,768]{2,1,0:T(8,128)(2,1)S(1)} %copy-done.1, bf16[1,2304,768]{2,1,0:T(8,128)(2,1)} %get-tuple-element.36), kind=kLoop, calls=%fused_computation.26 | loop fusion | flops 14155775 | bytes 7077892 | tf_op jit(solution)/shard_map/reduce_sum | solution.py:134
  355.3 0.0 copy-start
  355.3 25.0 %fusion.17 = (bf16[2,2304,768]{2,1,0:T(8,128)(2,1)}, f32[2,2304,768]{2,1,0:T(8,128)}, f32[2,2304,768]{2,1,0:T(8,128)}) fusion(bf16[2,2304,768]{2,1,0:T(8,128)(2,1)} %wd_ref.1, f32[]{:T(128)S(6)} %min_shard_map.3, bf16[1,2304,768]{2,1,0:T(8,128)(2,1)} %get-tuple-element.35, bf16[1,2304,768]{2,1,0:T(8,128)(2,1)} %get-tuple-element.36, ...), kind=kLoop, calls=%fused_computation.32 | loop fusion | flops 70778880 | bytes 77856768 | tf_op jit(solution)/shard_map/convert_element_type | solution.py:118
  380.2 0.0 copy-done
  380.3 47.5 %fusion.8 = (bf16[2,768,2304]{2,1,0:T(8,128)(2,1)}, f32[2,768,2304]{2,1,0:T(8,128)}, f32[2,768,2304]{2,1,0:T(8,128)}, bf16[2,768,2304]{2,1,0:T(8,128)(2,1)}, f32...) fusion(bf16[2,768,2304]{2,1,0:T(8,128)(2,1)} %wg_h.1, f32[]{:T(128)S(6)} %min_shard_map.3, ...), kind=kLoop, calls=%fused_computation.23 | loop fusion | flops 141557760 | bytes 155713536 | tf_op jit(solution)/shard_map/convert_element_type | solution.py:118
Async XLA Ops:
  7.2 325.1 %all-reduce.3.cloned.1.call-start = ((), (), s32[]{:S(2)}) async-start(), calls=%async_computation | async-start | bytes 42467328 | tf_op jit(solution)/shard_map/psum | solution.py:132
  332.2 16.1 %copy-start.1 = (bf16[1,2304,768]{2,1,0:T(8,128)(2,1)S(1)}, bf16[1,2304,768]{2,1,0:T(8,128)(2,1)}, u32[]{:S(2)}) copy-start(bf16[1,2304,768]{2,1,0:T(8,128)(2,1)} %get-tuple-element.35) | copy-start | bytes 10616836
  355.3 25.0 %copy-start = (bf16[1,768,2304]{2,1,0:T(8,128)(2,1)S(1)}, bf16[1,768,2304]{2,1,0:T(8,128)(2,1)}, u32[]{:S(2)}) copy-start(bf16[1,768,2304]{2,1,0:T(8,128)(2,1)} %get-tuple-element.31) | copy-start | bytes 10616836
Sparse Core Ops, SparseCore 0:
  150.1 182.1 all-reduce.2

commit v2 on v1

v2 whole, which is shorter than its diff:
```python
import functools
import jax, jax.numpy as jnp
from jax import lax
from jax.experimental import pallas as pl
from jax.experimental.pallas import tpu as pltpu
from jax.sharding import PartitionSpec as P
F32,BF=jnp.float32,jnp.bfloat16
ANY=pl.BlockSpec(memory_space=pl.ANY)
VM=pl.BlockSpec(memory_space=pltpu.VMEM)
def dot(a,b,dims=((1,),(0,))):
    return lax.dot_general(a,b,(dims,((),())),preferred_element_type=F32)
NT=((1,),(1,)); TN=((0,),(0,))
def norm_scale(wide): return lax.rsqrt(jnp.mean(wide*wide,-1,keepdims=True)+1e-6)
def normed(h):
    wide=h.astype(F32); return (wide*norm_scale(wide)).astype(BF)
def sigmoid(g): return 0.5*jnp.tanh(0.5*g)+0.5

def k1_body(x_ref,wg,wu,wd,gate_ref,up_ref,h_ref,a_ref,act,*,fc):
    x=x_ref[...]; a=normed(x); F=wg.shape[1]
    for c in range(F//fc):
        s=pl.ds(c*fc,fc)
        g=dot(a,wg[:,s]); u=dot(a,wu[:,s])
        gate_ref[:,s]=g; up_ref[:,s]=u
        act[:,s]=(g*sigmoid(g)*u).astype(BF)
    d=dot(act[...],wd[...]).astype(BF)
    h=(x.astype(F32)+d.astype(F32)).astype(BF)
    h_ref[...]=h; a_ref[...]=normed(h)
def k1(x,wg,wu,wd,bm=512,fc=768):
    T,D=x.shape; F=wg.shape[2]
    wspec=lambda r,c:pl.BlockSpec((None,r,c),lambda i:(0,0,0),pipeline_mode=pl.Buffered(1))
    row=lambda c:pl.BlockSpec((bm,c),lambda i:(i,0))
    return pl.pallas_call(functools.partial(k1_body,fc=fc),grid=(T//bm,),
        in_specs=[row(D),wspec(D,F),wspec(D,F),wspec(F,D)],
        out_specs=[row(F),row(F),row(D),row(D)],
        out_shape=[jax.ShapeDtypeStruct((T,F),F32)]*2+[jax.ShapeDtypeStruct((T,D),BF)]*2,
        scratch_shapes=[pltpu.VMEM((bm,F),BF)],
        compiler_params=pltpu.CompilerParams(vmem_limit_bytes=60<<20),name="k1",
        cost_estimate=pl.CostEstimate(flops=6*T*D*F,bytes_accessed=10*T*F,transcendentals=T*F))(x,wg,wu,wd)


MESH=pl.DeviceIdType.MESH
DMA=pltpu.SemaphoreType.DMA

class Shards:
    def __init__(s,n,D,F,ft):
        s.n=n; s.side=round((n//2)**0.5); s.D,s.F,s.ft=D,F,ft; s.nf=F//ft
        s.rg=D//n; s.rd=ft//n; s.nb=D//ft; s.rt=2*s.rg+s.rd*s.nb
        assert 2*s.side*s.side==n and s.rg*n==D and s.rd*n==ft and s.nb*ft==D

class Comm:
    NAMES=("loc","rc","f1","f2","fv","su1","su2","sv","own","P","sq","cS","cR","u1S","u1R","u2S","u2R","vS","vR","wS","wR","x1S","x1R","x2S","x2R","cgS","cgR","lS")
    @staticmethod
    def scratch(z,nl):
        S,nf,blk=z.side,z.nf,(z.rt,z.ft)
        V=lambda *s,dt=BF:pltpu.VMEM(s+blk,dt)
        h=S//2
        return [V(nl,2,S,S),V(nf,S,S),V(nf,2,h),V(nf,2,S),V(nf,S-1),V(2,S),V(2,2,S),V(2,S),V(2,dt=F32),V(nf,S),pltpu.VMEM(blk,F32),
            DMA((nf,)),DMA((nf,)),DMA((nf,2)),DMA((nf,2)),DMA((nf,2)),DMA((nf,2)),DMA((nf,S-1)),DMA((nf,S-1)),
            DMA((nf,S-1)),DMA((nf,S-1)),DMA((nf,2)),DMA((nf,2)),DMA((nf,2)),DMA((nf,2)),DMA((nf,)),DMA((nf,)),DMA((nf,))]
    STAGES=9
    def __init__(s,z,nl,refs,Q):
        s.z,s.nl,s.Q=z,nl,Q
        for nm,r in zip(s.NAMES,refs,strict=True): setattr(s,nm,r)
        me=lax.axis_index("dp"); S=z.side
        c=me%2; y=(me//2)%S; x=me//(2*S)
        s.me,s.c=me,c; s.u=x*(1-c)+y*c; s.v=y*(1-c)+x*c
        s.partner=me+1-2*c
        s.right=s.dev(s.u+1,s.v); s.left=s.dev(s.u+S-1,s.v)
        s.vpeer=[s.dev(s.u,s.v+d) for d in range(1,S)]
    def dev(s,u,v):
        S,c=s.z.side,s.c; u,v=u%S,v%S
        return ((u*(1-c)+v*c)*S+v*(1-c)+u*c)*2+c
    def greet(s,extra=()):
        b=pltpu.get_barrier_semaphore()
        for d in (s.partner,s.right,s.left,*s.vpeer,*extra): pl.semaphore_signal(b,inc=1,device_id={"dp":d},device_id_type=MESH)
    def met(s,extra=0):
        pl.semaphore_wait(pltpu.get_barrier_semaphore(),3+len(s.vpeer)+extra)
    def cp(s,src,dst,a,b,dev):
        return pltpu.make_async_remote_copy(src_ref=src,dst_ref=dst,send_sem=a,recv_sem=b,device_id={"dp":dev},device_id_type=MESH)
    def copies(s,i,k):
        S=s.z.side; h=S//2; n=lax.rem(k,s.nl); p=lax.rem(k,2); u,v,c=s.u,s.v,s.c
        ul,ur=(u+S-1)%S,(u+1)%S
        if i==0: return [s.cp(s.loc.at[n,1-c],s.rc.at[k],s.cS.at[k],s.cR.at[k],s.partner)]
        if i==1: return [s.cp(s.su1.at[p,pl.ds(0,h)],s.f1.at[k,0],s.u1S.at[k,0],s.u1R.at[k,0],s.right),
                         s.cp(s.su1.at[p,pl.ds(h,h)],s.f1.at[k,1],s.u1S.at[k,1],s.u1R.at[k,1],s.left)]
        if i==2: return [s.cp(s.su2.at[p,0],s.f2.at[k,0],s.u2S.at[k,0],s.u2R.at[k,0],s.right),
                         s.cp(s.su2.at[p,1],s.f2.at[k,1],s.u2S.at[k,1],s.u2R.at[k,1],s.left)]
        if i==3: return [s.cp(s.sv.at[p,(v+d)%S],s.fv.at[k,d-1],s.vS.at[k,d-1],s.vR.at[k,d-1],s.vpeer[d-1]) for d in range(1,S)]
        if i==4: return [s.cp(s.P.at[k,v],s.P.at[k,v],s.wS.at[k,d-1],s.wR.at[k,d-1],s.vpeer[d-1]) for d in range(1,S)]
        if i==5: return [s.cp(s.P.at[k],s.Q.at[c,k,u],s.x1S.at[k,0],s.x1R.at[k,0],s.right),
                         s.cp(s.P.at[k],s.Q.at[c,k,u],s.x1S.at[k,1],s.x1R.at[k,1],s.left)]
        if i==6: return [s.cp(s.Q.at[c,k,ul,pl.ds(0,h)],s.Q.at[c,k,ul,pl.ds(0,h)],s.x2S.at[k,0],s.x2R.at[k,0],s.right),
                         s.cp(s.Q.at[c,k,ur,pl.ds(h,h)],s.Q.at[c,k,ur,pl.ds(h,h)],s.x2S.at[k,1],s.x2R.at[k,1],s.left)]
        if i==7: return [s.cp(s.Q.at[c,k],s.Q.at[c,k],s.cgS.at[k],s.cgR.at[k],s.partner)]
    def arrived(s,i,k):
        S=s.z.side; h=S//2; u,v,c=s.u,s.v,s.c
        if i==4: return [s.cp(s.P.at[k,v],s.P.at[k,(v+S-d)%S],s.wS.at[k,d-1],s.wR.at[k,d-1],s.vpeer[d-1]) for d in range(1,S)]
        if i==5: return [s.cp(s.P.at[k],s.Q.at[c,k,(u+S-1)%S],s.x1S.at[k,0],s.x1R.at[k,0],s.right),
                         s.cp(s.P.at[k],s.Q.at[c,k,(u+1)%S],s.x1S.at[k,1],s.x1R.at[k,1],s.left)]
        if i==6:
            o=(u+h)%S
            return [s.cp(s.Q.at[c,k,o,pl.ds(0,h)],s.Q.at[c,k,o,pl.ds(0,h)],s.x2S.at[k,0],s.x2R.at[k,0],s.right),
                    s.cp(s.Q.at[c,k,o,pl.ds(h,h)],s.Q.at[c,k,o,pl.ds(h,h)],s.x2S.at[k,1],s.x2R.at[k,1],s.left)]
        if i==7: return [s.cp(s.Q.at[c,k],s.Q.at[1-c,k],s.cgS.at[k],s.cgR.at[k],s.partner)]
        return s.copies(i,k)
    def keep(s,k): return pltpu.make_async_copy(s.P.at[k],s.Q.at[s.c,k,s.u],s.lS.at[k])
    def stage(s,i,k):
        S=s.z.side; h=S//2; n=lax.rem(k,s.nl); p=lax.rem(k,2); u,v,c=s.u,s.v,s.c
        if i>0:
            for d in s.arrived(i-1,k): d.wait_recv()
            for d in s.copies(i-1,k): d.wait_send()
        f=lambda r:r[...].astype(F32)
        both=lambda q,sl:f(s.loc.at[n,c,q,sl])+f(s.rc.at[k,q,sl])
        A,B,al=pl.ds(0,h),pl.ds(h,h),pl.ds(0,S)
        if i==1:
            s.su1[p]=both((u+h)%S,al).astype(BF)
        if i==2:
            r,l=(u+1)%S,(u+S-1)%S
            s.su2[p,0,A]=(both(r,A)+f(s.f1.at[k,0])).astype(BF); s.su2[p,0,B]=both(r,B).astype(BF)
            s.su2[p,1,A]=both(l,A).astype(BF); s.su2[p,1,B]=(both(l,B)+f(s.f1.at[k,1])).astype(BF)
        if i==3:
            one=lambda r:f(s.loc.at[n,c,u,r])+f(s.rc.at[k,u,r])+f(s.f2.at[k,0,r])+f(s.f2.at[k,1,r])
            for d in range(1,S): s.sv[p,(v+d)%S]=one((v+d)%S).astype(BF)
            s.own[p]=one(v)
        if i==4:
            g=s.own[p]
            for d in range(S-1): g=g+f(s.fv.at[k,d])
            g=g.astype(BF); s.P[k,v]=g
            g=g.astype(F32); s.sq[...]+=g*g
        if i==5: s.keep(k).start()
        if i==7: s.keep(k).wait()
        if i<8:
            for d in s.copies(i,k): d.start()
    def point(s,stages,chunk):
        for i in stages:
            k=chunk(i)
            @pl.when((k>=0)&(k<s.z.nf))
            def _(i=i,k=k): s.stage(i,k)
    def store(s,k,a,part):
        z=s.z; S=z.side; n=lax.rem(k,s.nl)
        for i in range(z.n):
            at=(n,i//(S*S),i//S%S,i%S)
            if part<2: s.loc[(*at,pl.ds(part*z.rg,z.rg))]=a[i*z.rg:(i+1)*z.rg].astype(BF)
            else:
                for b in range(z.nb): s.loc[(*at,pl.ds(2*z.rg+b*z.rd,z.rd))]=a[i*z.rd:(i+1)*z.rd,b*z.ft:(b+1)*z.ft].astype(BF)

def elementwise(g,u,da):
    sg=sigmoid(g); silu=g*sg
    return (silu*u).astype(BF),(da*u*(sg+silu*(1.0-sg))).astype(BF),(da*silu).astype(BF)

def k2_body(a_ref,dy_ref,h_ref,wg_h,wu_h,wd_h,Q,ss_ref,dh_ref,wg,wu,wd,aT,dg,du,act,sem,*refs,z,nl,rc,bc,L):
    j=pl.program_id(0); T,D=a_ref.shape; nf,ft=z.nf,z.ft
    m=Comm(z,nl,refs,Q)
    def cps(t):
        s=pl.ds(pl.multiple_of(t*ft,ft),ft)
        return [pltpu.make_async_copy(wg_h.at[L,:,s],wg.at[:,s],sem.at[0,t]),pltpu.make_async_copy(wu_h.at[L,:,s],wu.at[:,s],sem.at[1,t]),
                pltpu.make_async_copy(wd_h.at[L,s,:],wd.at[lax.rem(t,2)],sem.at[2,t])]
    @pl.when(j==0)
    def _():
        m.greet()
        for c in cps(0): c.start()
        for t in range(1,nf):
            for c in cps(t)[:2]: c.start()
        m.sq[...]=jnp.zeros_like(m.sq)
        for r in range(0,T,rc): aT[:,pl.ds(r,rc)]=a_ref[pl.ds(r,rc),:].T
    s=pl.ds(pl.multiple_of(lax.rem(j,nf)*ft,ft),ft)
    @pl.when(j<nf)
    def _():
        for c in cps(j): c.wait()
        @pl.when(j+1<nf)
        def _(): cps(j+1)[2].start()
        wgt,wut,wdt=wg[:,s],wu[:,s],wd[lax.rem(j,2)]
        for r in range(0,T,rc):
            rs=pl.ds(r,rc); a=a_ref[rs,:]
            g=dot(a,wgt); u=dot(a,wut); da=dot(dy_ref[rs,:],wdt,NT).astype(BF).astype(F32)
            act[rs,:],dg[rs,s],du[rs,s]=elementwise(g,u,da)
    @pl.when(j==0)
    def _(): m.met()
    m.point((1,3,5,7),lambda i:(2*j-1-i)//2)
    @pl.when(j<nf)
    def _():
        m.store(j,dot(aT[...],dg[:,s]),0)
        m.store(j,dot(aT[...],du[:,s]),1)
        m.store(j,dot(act[...],dy_ref[...],TN),2)
    @pl.when(j>=nf)
    def _():
        rs=pl.ds(pl.multiple_of((j-nf)*bc,bc),bc)
        da=(dot(dg[rs,:],wg[...],NT).astype(BF).astype(F32)+dot(du[rs,:],wu[...],NT).astype(BF).astype(F32)).astype(BF).astype(F32)
        wide=h_ref[...].astype(F32); sc=norm_scale(wide)
        t=jnp.sum(da*wide,-1,keepdims=True)*(1.0/D)
        dn=(da*sc-wide*(sc*sc*sc*t)).astype(BF).astype(F32)
        dh_ref[...]=(dy_ref[rs,:].astype(F32)+dn).astype(BF)
    m.point((0,2,4,6,8),lambda i:(2*j-i)//2)
    @pl.when(j==pl.num_programs(0)-1)
    def _(): ss_ref[...]=m.sq[...]
def k2(a1,dy,h1,wg,wu,wd,n,L,ft=256,rc=512,bc=512):
    T,D=a1.shape; F=wg.shape[2]; z=Shards(n,D,F,ft); nf=z.nf; nb=T//bc; nl=2; S=z.side
    assert 2*(nf-1)+1+8<=2*(nf+nb)-1
    back=pl.BlockSpec((bc,D),lambda j:(jnp.maximum(j-nf,0),0))
    return pl.pallas_call(functools.partial(k2_body,z=z,nl=nl,rc=rc,bc=bc,L=L),grid=(nf+nb,),
        in_specs=[VM,VM,back,ANY,ANY,ANY],out_specs=[ANY,pl.BlockSpec((z.rt,ft),lambda j:(0,0)),back],
        out_shape=[jax.ShapeDtypeStruct((2,nf,S,S,z.rt,ft),BF),jax.ShapeDtypeStruct((z.rt,ft),F32),jax.ShapeDtypeStruct((T,D),BF)],
        scratch_shapes=[pltpu.VMEM((D,F),BF),pltpu.VMEM((D,F),BF),pltpu.VMEM((2,ft,D),BF),pltpu.VMEM((D,T),BF),
                        pltpu.VMEM((T,F),BF),pltpu.VMEM((T,F),BF),pltpu.VMEM((T,ft),BF),DMA((3,nf)),*Comm.scratch(z,nl)],
        compiler_params=pltpu.CompilerParams(vmem_limit_bytes=67043328,collective_id=1,has_side_effects=True),name="k2",
        cost_estimate=pl.CostEstimate(flops=16*T*D*F,bytes_accessed=30<<20,transcendentals=T*F))(a1,dy,h1,wg,wu,wd)

def k3_body(x_ref,dh_ref,g_ref,u_ref,wd_ref,ss_ref,Q,f_ref,aT,dg,du,act,nsend,nv,nu,nc,nS,nR,*refs,z,nl,rc,count):
    j=pl.program_id(0); T,D=x_ref.shape; nf,S=z.nf,z.side
    m=Comm(z,nl,refs,Q); last=nf-1+m.STAGES-1
    upeer=[m.dev(m.u+d,m.v) for d in range(1,S)]; far=[upeer[d] for d in range(1,S-2)]
    @pl.when(j==0)
    def _():
        m.greet(far)
        m.sq[...]=ss_ref[...]
        for r in range(0,T,rc): aT[:,pl.ds(r,rc)]=normed(x_ref[pl.ds(r,rc),:]).T
    @pl.when(j<nf)
    def _():
        wdt=wd_ref[...]
        for r in range(0,T,rc):
            rs=pl.ds(r,rc)
            da=dot(dh_ref[rs,:],wdt,NT).astype(BF).astype(F32)
            act[rs,:],dg[rs,:],du[rs,:]=elementwise(g_ref[rs,:],u_ref[rs,:],da)
        m.store(j,dot(aT[...],dg[...]),0)
        m.store(j,dot(aT[...],du[...]),1)
        m.store(j,dot(act[...],dh_ref[...],TN),2)
    @pl.when(j==0)
    def _(): m.met(len(far))
    m.point(range(9),lambda i:j-i)
    def cps(buf,at,peers,b): return [m.cp(nsend.at[b],buf.at[at],nS.at[b,i],nR.at[b,i],p) for i,p in enumerate(peers)]
    def wait(buf,at,peers,b):
        for i in range(len(peers)):
            m.cp(nsend.at[b],buf.at[at[i]],nS.at[b,i],nR.at[b,i],peers[i]).wait()
    def total(ref,k):
        t=ref[0]
        for i in range(1,k): t=t+ref[i]
        return t
    @pl.when(j==last-3)
    def _():
        t=jnp.broadcast_to(jnp.sum(jnp.sum(m.sq[...],0,keepdims=True),1,keepdims=True),(8,128))
        nsend[0]=t; nv[m.v]=t
        for d in cps(nv,m.v,m.vpeer,0): d.start()
    @pl.when(j==last-2)
    def _():
        wait(nv,[(m.v+S-d)%S for d in range(1,S)],m.vpeer,0)
        t=total(nv,S); nsend[1]=t; nu[m.u]=t
        for d in cps(nu,m.u,upeer,1): d.start()
    @pl.when(j==last-1)
    def _():
        wait(nu,[(m.u+S-d)%S for d in range(1,S)],upeer,1)
        t=total(nu,S); nsend[2]=t; nc[m.c]=t
        for d in cps(nc,m.c,[m.partner],2): d.start()
    @pl.when(j==last)
    def _():
        wait(nc,[1-m.c],[m.partner],2)
        f_ref[...]=jnp.minimum(1.0,0.5*lax.rsqrt(total(nc,2)*(1.0/count)+1e-30))
def k3(x,dh,gate,up,wd,ss,n,L,count,ft=256,rc=512):
    T,D=x.shape; F=gate.shape[1]; z=Shards(n,D,F,ft); nf=z.nf; S=z.side; nl=4
    cl=lambda j:jnp.minimum(j,nf-1)
    col=lambda r:pl.BlockSpec((r,ft),lambda j:(0,cl(j)))
    return pl.pallas_call(functools.partial(k3_body,z=z,nl=nl,rc=rc,count=count),grid=(nf+Comm.STAGES-1,),
        in_specs=[VM,VM,col(T),col(T),pl.BlockSpec((None,ft,D),lambda j:(L,cl(j),0)),VM],
        out_specs=[ANY,pl.BlockSpec((8,128),lambda j:(0,0))],
        out_shape=[jax.ShapeDtypeStruct((2,nf,S,S,z.rt,ft),BF),jax.ShapeDtypeStruct((8,128),F32)],
        scratch_shapes=[pltpu.VMEM((D,T),BF)]+[pltpu.VMEM((T,ft),BF)]*3+[pltpu.VMEM((3,8,128),F32),pltpu.VMEM((S,8,128),F32),pltpu.VMEM((S,8,128),F32),
            pltpu.VMEM((2,8,128),F32),DMA((3,S-1)),DMA((3,S-1)),*Comm.scratch(z,nl)],
        compiler_params=pltpu.CompilerParams(vmem_limit_bytes=67043328,collective_id=2,has_side_effects=True),name="k3",
        cost_estimate=pl.CostEstimate(flops=8*T*D*F,bytes_accessed=10*T*F,transcendentals=T*F))(x,dh,gate,up,wd,ss)

def adam_body(f_ref,g1,g0,*refs,z,half):
    ins,outs=refs[:9],refs[9:]
    i=pl.program_id(0); S,ft,rg,rd,nb=z.side,z.ft,z.rg,z.rd,z.nb
    f=f_ref[0:1,0:1]
    def one(g,w,m,v,wo,mo,vo,at):
        g=g.astype(F32)*f
        m=0.9*m[at]+0.1*g
        v=0.95*v[at]+0.05*g*g
        w=w[at].astype(F32)
        wo[at]=(w-0.02*(m*lax.rsqrt(v+1e-8)+0.1*w)).astype(BF); mo[at]=m; vo[at]=v
    def piece(q):
        def tile(t,_):
            cs=pl.ds(pl.multiple_of(t*ft,ft),ft)
            for r in range(S):
                for a in range(2):
                    one(q[t,r,pl.ds(a*rg,rg),:],*(ins[a+3*b] for b in range(3)),*(outs[a+3*b] for b in range(3)),(pl.ds(r*rg,rg),cs))
                for b in range(nb):
                    one(q[t,r,pl.ds(2*rg+b*rd,rd),:],*(ins[2+3*b_] for b_ in range(3)),*(outs[2+3*b_] for b_ in range(3)),(t,pl.ds(r*rd,rd),pl.ds(b*ft,ft)))
            return _
        lax.fori_loop(0,z.nf,tile,0)
    @pl.when(i<half)
    def _(): piece(g1)
    @pl.when(i>=half)
    def _(): piece(g0)
def adam(f,G1,G0,w,m,v,n,ft=256):
    L,D,F=w[0].shape; z=Shards(n,D,F,ft); S,nf=z.side,z.nf; hf=2*S; rows=D//hf
    one=lambda a:a.reshape(L*hf,rows,F)
    dn=lambda a:a.reshape(L,nf,hf,ft//hf,D)
    args=[(dn if k==2 else one)(a) for t in (w,m,v) for k,a in enumerate(t)]
    lay=lambda i:1-i//hf
    bo=pl.BlockSpec((None,rows,F),lambda i:(lay(i)*hf+i%hf,0,0)); bd=pl.BlockSpec((None,nf,None,ft//hf,D),lambda i:(lay(i),0,i%hf,0,0))
    g1=lambda i:(jnp.minimum(i,hf-1)); g0=lambda i:jnp.maximum(i-hf,0)
    gs=lambda k:pl.BlockSpec((None,nf,None,S,z.rt,ft),lambda i:(k(i)//S,0,k(i)%S,0,0,0))
    specs=[bo,bo,bd]*3
    out=pl.pallas_call(functools.partial(adam_body,z=z,half=hf),grid=(L*hf,),
        in_specs=[pl.BlockSpec((8,128),lambda i:(0,0)),gs(g1),gs(g0)]+specs,out_specs=specs,
        out_shape=[jax.ShapeDtypeStruct(a.shape,a.dtype) for a in args],
        compiler_params=pltpu.CompilerParams(vmem_limit_bytes=56<<20),name="adamw",
        cost_estimate=pl.CostEstimate(flops=60*L*D*F,bytes_accessed=66*L*D*F,transcendentals=3*L*D*F))(f,G1,G0,*args)
    return [o.reshape(a.shape) for o,a in zip(out,[*w,*m,*v])]

def solution(mesh):
    n=mesh.shape["dp"]
    def step(x,dy,*arrays):
        w,m,v=(arrays[i:i+3] for i in (0,3,6))
        count=sum(a.size for a in w)
        gate,up,h1,a1=k1(x[0],*w)
        G1,ss,dh=k2(a1,dy[0],h1,*w,n,1)
        G0,f=k3(x[0],dh,gate,up,w[2],ss,n,0,count)
        return tuple(adam(f,G1,G0,w,m,v,n))
    return jax.shard_map(step,mesh=mesh,in_specs=(P(("rep","dp"),None,None),)*2+(P(None,None,None),)*9,
        out_specs=(P("rep",None,None),)*9,check_vma=False)
```

time: 435 us -> 336 us (0.77)
  Pallas kernels: 143 us -> 335 us
  waiting for transfers between devices: 182 us -> 0 us
  other arithmetic: 93.5 us -> 0 us
  between operations: 16.1 us -> 0.83 us
    pallas_call x2 -> x3, Pallas kernels: 112 us -> 305 us  [the longest x1 126 us: k2(): pl.pallas_call(functools.partial(k2_body, z=z, nl=nl, rc=rc, bc=bc, L=L),...]
    psum x1 -> x0, waiting for transfers between devices: 182 us -> none  [step(): summed = [[lax.psum(g, 'dp') for g in one] for one in (of0, of1)]]
    convert_element_type x2 -> x0, other arithmetic: 72.4 us -> none  [adamw(): return ((w - 0.02 * step).astype(jnp.bfloat16), m, v)]
    reduce_sum x3 -> x0, other arithmetic: 21 us -> none  [step(): jnp.sum(g * g)]
  transfers between devices with their start and end apart: 1 -> 0, of which waited for: 1 -> 0; matrix products, arithmetic and copies ran while one was open for 0% -> 0% of each run, Pallas kernels for 0% -> 0%
where the time goes in v2:
time: 336 us
  Pallas kernels  335 us (100%)
    pallas_call x1, Pallas kernels, k2(): pl.pallas_call(functools.partial(k2_body, z=z, nl=nl, rc=rc, bc=bc, L=L),...  126 us
    pallas_call x1, Pallas kernels, k3(): pl.pallas_call(functools.partial(k3_body, z=z, nl=nl, rc=rc, count=count)...  99.9 us
    pallas_call x1, Pallas kernels, adam(): pl.pallas_call(functools.partial(adam_body, z=z, half=hf), grid=(L * hf,)...  78.7 us
    pallas_call x1, Pallas kernels, k1(): pl.pallas_call(functools.partial(k1_body, fc=fc), grid=(T // bm,), in_spe...  30.8 us

profile of v2, /device:TPU:97, one launch (start us, length us, event | category | flops | bytes accessed | tf_op | source)
XLA Modules:
  0.0 336.2 jit_solution(6723101064357892945)
XLA Ops:
  0.6 30.8 %k1.1 = (f32[2048,2304]{1,0:T(8,128)}, f32[2048,2304]{1,0:T(8,128)}, bf16[2048,768]{1,0:T(8,128)(2,1)}, bf16[2048,768]{1,0:T(8,128)(2,1)}) custom-call(bf16[2048,768]{1,0:T(8,128)(2,1)} %bitcast.39, bf16[2,768,2304]{2,1,0:T(8,128)(2,1)} %wg_h.1, bf16[2,768,2304]{2,1,0:T(8,128)(2,1)} %wu_h.1, bf16[2,2304,768]{2,1,0:T(8,128)(2,1)} %wd_ref.1), custom_call_target="tpu_custom_call" | custom-call | flops 21743271936 | bytes 47185920 | tf_op jit(solution)/shard_map/k1/pallas_call | solution.py:32
  31.5 125.8 %k2.1 = (bf16[2,9,4,4,72,256]{5,4,3,2,1,0:T(8,128)(2,1)}, f32[72,256]{1,0:T(8,128)}, bf16[2048,768]{1,0:T(8,128)(2,1)}) custom-call(bf16[2048,768]{1,0:T(8,128)(2,1)} %get-tuple-element.27.a_ref, bf16[2048,768]{1,0:T(8,128)(2,1)} %bitcast.38, bf16[2048,768]{1,0:T(8,128)(2,1)} %get-tuple-element.28.h_ref, bf16[2,768,2304]{2,1,0:T(8,128)(2,1)} %wg_h.1, ...), custom_call_target="tpu_custom_call" | custom-call | flops 57982058496 | bytes 31457280 | tf_op jit(solution)/shard_map/k2/pallas_call | solution.py:200
  157.3 99.9 %k3.1 = (bf16[2,9,4,4,72,256]{5,4,3,2,1,0:T(8,128)(2,1)}, f32[8,128]{1,0:T(8,128)}) custom-call(bf16[2048,768]{1,0:T(8,128)(2,1)} %bitcast.40, bf16[2048,768]{1,0:T(8,128)(2,1)} %get-tuple-element.29.dh_ref, f32[2048,2304]{1,0:T(8,128)} %get-tuple-element.30.g_ref, f32[2048,2304]{1,0:T(8,128)} %get-tuple-element.31.u_ref, bf16[2,2304,768]{2,1,0:T(8,128)(2,1)} %wd_ref.1, ...), custom_call_target="tpu_custom_call" | custom-call | flops 28991029248 | bytes 47185920 | tf_op jit(solution)/shard_map/k3/pallas_call | solution.py:261
  257.3 78.7 %adamw.1 = (bf16[16,96,2304]{2,1,0:T(8,128)(2,1)}, bf16[16,96,2304]{2,1,0:T(8,128)(2,1)}, bf16[2,9,8,32,768]{4,3,2,1,0:T(8,128)(2,1)}, f32[16,96,2304]{2,1,0:T(8...) custom-call(f32[8,128]{1,0:T(8,128)} %get-tuple-element.33.f_ref, ...), custom_call_target="tpu_custom_call" | custom-call | flops 212336640 | bytes 233570304 | tf_op jit(solution)/shard_map/adamw/pallas_call | solution.py:304

commit v3 on v0

v3 whole, which is shorter than its diff:
```python
import functools
import jax, jax.numpy as jnp
from jax import lax
from jax.experimental import pallas as pl
from jax.experimental.pallas import tpu as pltpu
from jax.sharding import PartitionSpec
F32,BF=jnp.float32,jnp.bfloat16
ANY=pl.BlockSpec(memory_space=pl.ANY)
VM=pl.BlockSpec(memory_space=pltpu.VMEM)
def dot(a,b,dims=((1,),(0,))):
    return lax.dot_general(a,b,(dims,((),())),preferred_element_type=F32)
NT=((1,),(1,)); TN=((0,),(0,))
def norm_scale(wide): return lax.rsqrt(jnp.mean(wide*wide,-1,keepdims=True)+1e-6)
def normed(h):
    wide=h.astype(F32); return (wide*norm_scale(wide)).astype(BF)
def sigmoid(g): return 0.5*jnp.tanh(0.5*g)+0.5

def k1_body(x_ref,wg,wu,wd,gate_ref,up_ref,h_ref,a_ref,aT_ref,act,*,fc):
    x=x_ref[...]; a=normed(x); F=wg.shape[1]; aT_ref[...]=a.T
    for c in range(F//fc):
        s=pl.ds(c*fc,fc)
        g=dot(a,wg[:,s]); u=dot(a,wu[:,s])
        gate_ref[:,s]=g; up_ref[:,s]=u
        act[:,s]=(g*sigmoid(g)*u).astype(BF)
    d=dot(act[...],wd[...]).astype(BF)
    h=(x.astype(F32)+d.astype(F32)).astype(BF)
    h_ref[...]=h; a_ref[...]=normed(h)
def k1(x,wg,wu,wd,bm=512,fc=768):
    T,D=x.shape; F=wg.shape[2]
    wspec=lambda r,c:pl.BlockSpec((None,r,c),lambda i:(0,0,0),pipeline_mode=pl.Buffered(1))
    row=lambda c:pl.BlockSpec((bm,c),lambda i:(i,0))
    return pl.pallas_call(functools.partial(k1_body,fc=fc),grid=(T//bm,),
        in_specs=[row(D),wspec(D,F),wspec(D,F),wspec(F,D)],
        out_specs=[row(F),row(F),row(D),row(D),pl.BlockSpec((D,bm),lambda i:(0,i))],
        out_shape=[jax.ShapeDtypeStruct((T,F),F32)]*2+[jax.ShapeDtypeStruct((T,D),BF)]*2+[jax.ShapeDtypeStruct((D,T),BF)],
        scratch_shapes=[pltpu.VMEM((bm,F),BF)],
        compiler_params=pltpu.CompilerParams(vmem_limit_bytes=60<<20),name="k1",
        cost_estimate=pl.CostEstimate(flops=6*T*D*F,bytes_accessed=10*T*F,transcendentals=T*F))(x,wg,wu,wd)


MESH=pl.DeviceIdType.MESH
DMA=pltpu.SemaphoreType.DMA
LANES=128

class Shards:
    def __init__(s,n,D,F,ft):
        s.n=n; s.side=round((n//2)**0.5); s.D,s.F,s.ft=D,F,ft; s.nf=F//ft
        s.rg=D//n; s.rd=ft//n; s.part=s.rg*ft//LANES; s.blk=(3*s.part,LANES)
        assert 2*s.side*s.side==n and s.rg*n==D and s.rd*n==ft and ft%LANES==0 and D%LANES==0

class Place:
    def __init__(s,S):
        me=lax.axis_index("dp"); c=me%2; y=(me//2)%S; x=me//(2*S)
        s.S,s.c,s.u,s.v=S,c,x*(1-c)+y*c,y*(1-c)+x*c
        s.partner=me+1-2*c; s.right=s.dev(s.u+1,s.v); s.left=s.dev(s.u+S-1,s.v)
        s.vpeer=[s.dev(s.u,s.v+d) for d in range(1,S)]; s.upeer=[s.dev(s.u+d,s.v) for d in range(1,S)]
    def place(s,layer,other,d):
        S,c=s.S,s.c; return (layer*2+(1-c if other else c))*S+((s.v if other else s.u)+S-d)%S
    def dev(s,u,v):
        S,c=s.S,s.c; u,v=u%S,v%S
        return ((u*(1-c)+v*c)*S+v*(1-c)+u*c)*2+c
    def greet(s,peers):
        b=pltpu.get_barrier_semaphore()
        for d in peers: pl.semaphore_signal(b,inc=1,device_id={"dp":d},device_id_type=MESH)

def send(src,dst,a,b,dev):
    return pltpu.make_async_remote_copy(src_ref=src,dst_ref=dst,send_sem=a,recv_sem=b,device_id={"dp":dev},device_id_type=MESH)
def wide(r): return r[...].astype(F32)

class Scatter:
    N=13
    @staticmethod
    def scratch(z,nl,ns):
        S,nf,blk=z.side,z.nf,z.blk
        V=lambda *s,dt=BF:pltpu.VMEM(s+blk,dt)
        return [V(nl,2,S,S),V(nf,S,S),V(nf,S-1,S),V(nf,S-1),V(ns,S-1,S),V(ns,S-1),V(ns,dt=F32),DMA((nf,)),DMA((nf,)),*[DMA((nf,S-1))]*4]
    def __init__(s,z,pos,nl,ns,refs):
        s.z,s.pos,s.nl,s.ns=z,pos,nl,ns
        (s.loc,s.rc,s.fu,s.fv,s.su,s.sv,s.own,s.cS,s.cR,s.uS,s.uR,s.vS,s.vR)=refs
    def copies(s,i,k):
        o=s.pos; n=lax.rem(k,s.nl); p=lax.rem(k,s.ns)
        if i==0: return [send(s.loc.at[n,1-o.c],s.rc.at[k],s.cS.at[k],s.cR.at[k],o.partner)]
        if i==1: return [send(s.su.at[p,d],s.fu.at[k,d],s.uS.at[k,d],s.uR.at[k,d],to) for d,to in enumerate(o.upeer)]
        if i==2: return [send(s.sv.at[p,d],s.fv.at[k,d],s.vS.at[k,d],s.vR.at[k,d],to) for d,to in enumerate(o.vpeer)]
    def step(s,i,k,done=None):
        o=s.pos; S=o.S; n=lax.rem(k,s.nl); p=lax.rem(k,s.ns); u,v,c=o.u,o.v,o.c
        if i>0:
            for d in s.copies(i-1,k): d.wait()
        both=lambda q,sl:wide(s.loc.at[n,c,q,sl])+wide(s.rc.at[k,q,sl])
        if i==1:
            for d in range(S-1): s.su[p,d]=both((u+d+1)%S,pl.ds(0,S)).astype(BF)
        if i==2:
            def one(r):
                t=both(u,r)
                for d in range(S-1): t=t+wide(s.fu.at[k,d,r])
                return t
            for d in range(S-1): s.sv[p,d]=one((v+d+1)%S).astype(BF)
            s.own[p]=one(v)
        if i==3:
            g=s.own[p]
            for d in range(S-1): g=g+wide(s.fv.at[k,d])
            done(k,g.astype(BF))
        if i<3:
            for d in s.copies(i,k): d.start()
    def store(s,k,a,part):
        z=s.z; S=z.side; n=lax.rem(k,s.nl); r=z.rd if part==2 else z.rg
        for i in range(z.n):
            rows=a[i*r:(i+1)*r]
            s.loc[n,i//(S*S),i//S%S,i%S,pl.ds(part*z.part,z.part)]=jnp.concatenate([rows[:,b:b+LANES] for b in range(0,a.shape[1],LANES)],0).astype(BF)

class Gather:
    N=10
    @staticmethod
    def scratch(z,count):
        S=z.side
        return [pltpu.VMEM((count,S,*z.blk),BF),*[DMA((count,S-1))]*2,*[DMA((count,2))]*4,*[DMA((count,))]*3]
    def __init__(s,z,pos,first,Q,refs):
        s.z,s.pos,s.first,s.Q=z,pos,first,Q
        (s.P,s.wS,s.wR,s.aS,s.aR,s.bS,s.bR,s.cS,s.cR,s.lS)=refs
    def copies(s,i,k,here=False):
        o=s.pos; S=o.S; h=S//2; u,v,c=o.u,o.v,o.c; q=k+s.first; l,r=(u+S-1)%S,(u+1)%S; P,Q=s.P,s.Q
        A,B=pl.ds(0,h),pl.ds(h,h)
        if i==0: return [send(P.at[k,v],P.at[k,(v+S-d)%S if here else v],s.wS.at[k,d-1],s.wR.at[k,d-1],o.vpeer[d-1]) for d in range(1,S)]
        if i==1: return [send(P.at[k],Q.at[c,q,(l,r)[w] if here else u],s.aS.at[k,w],s.aR.at[k,w],d) for w,d in enumerate((o.right,o.left))]
        if i==2: return [send(Q.at[c,q,(l,r)[w],(A,B)[w]],Q.at[c,q,(u+h)%S if here else (l,r)[w],(A,B)[w]],s.bS.at[k,w],s.bR.at[k,w],d) for w,d in enumerate((o.right,o.left))]
        if i==3: return [send(Q.at[c,q],Q.at[1-c if here else c,q],s.cS.at[k],s.cR.at[k],o.partner)]
    def keep(s,k): return pltpu.make_async_copy(s.P.at[k],s.Q.at[s.pos.c,k+s.first,s.pos.u],s.lS.at[k])
    def step(s,i,k):
        if i>0:
            for d in s.copies(i-1,k,True): d.wait()
        if i==1: s.keep(k).start()
        if i==3: s.keep(k).wait()
        if i<4:
            for d in s.copies(i,k): d.start()

def run(points,p,parity,do):
    if not any(t%2==parity for t in points): return
    upto=lambda q:sum((q>=t).astype(jnp.int32) for t in points)
    lax.fori_loop(upto(p-1),upto(p),lambda k,_:(do(k),0)[1],0)

def elementwise(g,u,da):
    sg=sigmoid(g); silu=g*sg
    return (silu*u).astype(BF),(da*u*(sg+silu*(1.0-sg))).astype(BF),(da*silu).astype(BF)

def check_points(rs,nl,ns,later):
    nf=len(rs)
    for k in range(nf):
        assert rs[k][0]==2*(k+later)+1 and all(a<b for a,b in zip(rs[k],rs[k][1:])),rs[k]
        if k>=nl: assert rs[k-nl][2]<2*(k+later)
        if k>=ns: assert all(rs[k-ns][i+1]<=rs[k][i] for i in (1,2))
        if k: assert all(a<=b for a,b in zip(rs[k-1],rs[k]))
def check_gather(ag,starts=None):
    for k,t in enumerate(ag):
        assert all(a<b for a,b in zip(t,t[1:])) and (not starts or t[0]==starts[k]),t
        if k: assert all(a<=b for a,b in zip(ag[k-1],t))

def k2_body(a_ref,dy_ref,h_ref,wg_h,wu_h,wd_h,Q,ss_ref,left_ref,dh_ref,wg,wu,wd,aT,dg,du,act,sem,*refs,z,nl,ns,rc,bc,L,rs,ag):
    j=pl.program_id(0); T,D=a_ref.shape; nf,ft=z.nf,z.ft; na=len(ag); nb=T//bc
    o=Place(z.side); sc=Scatter(z,o,nl,ns,refs[:Scatter.N]); ga=Gather(z,o,0,Q,refs[Scatter.N:])
    def done(k,g):
        w=g.astype(F32); ss_ref[...]+=w*w
        @pl.when(k<na)
        def _(): ga.P[k,o.v]=g; ga.step(0,k)
        if na<nf:
            @pl.when(k>=na)
            def _(): left_ref[k-na]=g
    def point(p,parity):
        for i in (3,2,1,0): run([t[i] for t in rs],p,parity,lambda k:sc.step(i,k,done))
        for i in (4,3,2,1): run([t[i] for t in ag],p,parity,lambda k:ga.step(i,k))
    def cps(t):
        s=pl.ds(pl.multiple_of(t*ft,ft),ft)
        return [pltpu.make_async_copy(wg_h.at[L,:,s],wg.at[:,s],sem.at[0,t]),pltpu.make_async_copy(wu_h.at[L,:,s],wu.at[:,s],sem.at[1,t]),
                pltpu.make_async_copy(wd_h.at[L,s,:],wd.at[lax.rem(t,2)],sem.at[2,t])]
    @pl.when(j==0)
    def _():
        o.greet((o.partner,*o.upeer,*o.vpeer))
        for c in cps(0): c.start()
        for t in range(1,nf):
            for c in cps(t)[:2]: c.start()
        ss_ref[...]=jnp.zeros_like(ss_ref)
        for r in range(0,T,rc): aT[:,pl.ds(r,rc)]=a_ref[pl.ds(r,rc),:].T
    s=pl.ds(pl.multiple_of(lax.rem(j,nf)*ft,ft),ft)
    @pl.when(j<nf)
    def _():
        for c in cps(j): c.wait()
        @pl.when(j+1<nf)
        def _(): cps(j+1)[2].start()
        wgt,wut,wdt=wg[:,s],wu[:,s],wd[lax.rem(j,2)]
        for r in range(0,T,rc):
            rs_=pl.ds(r,rc); a=a_ref[rs_,:]
            g=dot(a,wgt); u=dot(a,wut); da=dot(dy_ref[rs_,:],wdt,NT).astype(BF).astype(F32)
            act[rs_,:],dg[rs_,s],du[rs_,s]=elementwise(g,u,da)
    @pl.when(j==0)
    def _(): pl.semaphore_wait(pltpu.get_barrier_semaphore(),1+len(o.upeer)+len(o.vpeer))
    point(2*j,0)
    @pl.when(j<nf)
    def _():
        sc.store(j,dot(aT[...],dg[:,s]),0)
        sc.store(j,dot(aT[...],du[:,s]),1)
        sc.store(j,dot(act[...],dy_ref[...],TN),2)
    @pl.when((j>=nf)&(j<nf+nb))
    def _():
        rs_=pl.ds(pl.multiple_of((j-nf)*bc,bc),bc)
        da=(dot(dg[rs_,:],wg[...],NT).astype(BF).astype(F32)+dot(du[rs_,:],wu[...],NT).astype(BF).astype(F32)).astype(BF).astype(F32)
        x=h_ref[...].astype(F32); scale=norm_scale(x)
        t=jnp.sum(da*x,-1,keepdims=True)*(1.0/D)
        dn=(da*scale-x*(scale*scale*scale*t)).astype(BF).astype(F32)
        dh_ref[...]=(dy_ref[rs_,:].astype(F32)+dn).astype(BF)
    point(2*j+1,1)
def k2(a1,dy,h1,wg,wu,wd,n,L,points,ft=256,rc=512,bc=256,nl=4,ns=3):
    T,D=a1.shape; F=wg.shape[2]; z=Shards(n,D,F,ft); nf=z.nf; nb=T//bc; S=z.side
    rs,ag=points; steps=max(nf+nb,max(t[-1] for t in rs+ag)//2+1); check_points(rs,nl,ns,0); check_gather(ag,[t[3] for t in rs]); nleft=max(nf-len(ag),1)
    back=pl.BlockSpec((bc,D),lambda j:(jnp.clip(j-nf,0,nb-1),0)); all_=lambda *s:pl.BlockSpec(s,lambda j:(0,)*len(s))
    return pl.pallas_call(functools.partial(k2_body,z=z,nl=nl,ns=ns,rc=rc,bc=bc,L=L,rs=rs,ag=ag),grid=(steps,),
        in_specs=[VM,VM,back,ANY,ANY,ANY],out_specs=[ANY,all_(*z.blk),all_(nleft,*z.blk),back],
        out_shape=[jax.ShapeDtypeStruct((2,nf,S,S,*z.blk),BF),jax.ShapeDtypeStruct(z.blk,F32),jax.ShapeDtypeStruct((nleft,*z.blk),BF),jax.ShapeDtypeStruct((T,D),BF)],
        scratch_shapes=[pltpu.VMEM((D,F),BF),pltpu.VMEM((D,F),BF),pltpu.VMEM((2,ft,D),BF),pltpu.VMEM((D,T),BF),
                        pltpu.VMEM((T,F),BF),pltpu.VMEM((T,F),BF),pltpu.VMEM((T,ft),BF),DMA((3,nf)),*Scatter.scratch(z,nl,ns),*Gather.scratch(z,max(len(ag),1))],
        compiler_params=pltpu.CompilerParams(vmem_limit_bytes=67043328,collective_id=1,has_side_effects=True),name="k2",
        cost_estimate=pl.CostEstimate(flops=16*T*D*F,bytes_accessed=30<<20,transcendentals=T*F))(a1,dy,h1,wg,wu,wd)

def k3_body(aT_h,dh_ref,g_ref,u_ref,wd_ref,ss_ref,left_ref,Q1_,P_out,f_ref,Q1,P_ref,aT,dg,du,act,sq,nsend,nv,nu,nc,nS,nR,gS,gR,oS,sem,*refs,z,nl,ns,rc,count,rs,ag,left,sqp):
    j=pl.program_id(0); D,T=aT.shape; nf,S=z.nf,z.side
    o=Place(S); sc=Scatter(z,o,nl,ns,refs[:Scatter.N])
    nleft=len(left); gl=Gather(z,o,nf-nleft,Q1,refs[Scatter.N:]) if nleft else None
    to=lambda k,here=False:[send(P_ref.at[k,o.v],P_ref.at[k,(o.v+S-d)%S if here else o.v],gS.at[k,d-1],gR.at[k,d-1],o.vpeer[d-1]) for d in range(1,S)]
    def done(k,g):
        w=g.astype(F32); sq[...]+=w*w
        P_ref[k,o.v]=g
        for d in to(k): d.start()
    def there(k):
        for d in to(k,True): d.wait()
        give(k).start()
    give=lambda k:pltpu.make_async_copy(P_ref.at[k],P_out.at[k],oS.at[k])
    def reduce_(p,parity):
        for i in (3,2,1,0): run([t[i] for t in rs],p,parity,lambda k:sc.step(i,k,done))
    def rest(p,parity):
        if nleft:
            for i in (4,3,2,1,0): run([t[i] for t in left],p,parity,lambda k:gl.step(i,k))
        run([t[1] for t in ag],p,parity,there)
    load=pltpu.make_async_copy(aT_h,aT,sem)
    def front(rows,b):
        for r in rows:
            rs_=pl.ds(r,rc)
            da=dot(dh_ref[rs_,:],wd_ref[...],NT).astype(BF).astype(F32)
            act[b,rs_,:],dg[b,rs_,:],du[b,rs_,:]=elementwise(g_ref[rs_,:],u_ref[rs_,:],da)
    def back(k,part,b):
        if part<2: sc.store(k,dot(aT[...],(dg,du)[part][b]),part)
        else: sc.store(k,dot(act[b],dh_ref[...],TN),2)
    rows=range(0,T,rc); half=len(rows)//2; b=lax.rem(j,2)
    @pl.when(j==0)
    def _():
        load.start()
        o.greet((o.partner,*o.upeer,*o.vpeer))
        sq[...]=ss_ref[...]
        for k in range(nleft): gl.P[k,o.v]=left_ref[k]
        front(rows[:half],b)
    @pl.when((j>0)&(j<nf))
    def _():
        front(rows[:half],b); back(j-1,0,1-b)
    @pl.when(j==nf)
    def _(): back(j-1,0,1-b)
    @pl.when(j==0)
    def _(): pl.semaphore_wait(pltpu.get_barrier_semaphore(),1+len(o.upeer)+len(o.vpeer))
    reduce_(2*j,0); rest(2*j,0)
    @pl.when(j==0)
    def _():
        front(rows[half:],b); load.wait()
    @pl.when((j>0)&(j<nf))
    def _():
        back(j-1,1,1-b); front(rows[half:],b); back(j-1,2,1-b)
    @pl.when(j==nf)
    def _(): back(j-1,1,1-b); back(j-1,2,1-b)
    p=2*j+1
    reduce_(p,1)
    def sums(buf,at,peers,b): return [send(nsend.at[b],buf.at[a],nS.at[b,i],nR.at[b,i],d) for i,(a,d) in enumerate(zip(at,peers))]
    def total(ref,k):
        t=ref[0]
        for i in range(1,k): t=t+ref[i]
        return t
    hops=((nv,o.v,o.vpeer,[(o.v+S-d)%S for d in range(1,S)],S),(nu,o.u,o.upeer,[(o.u+S-d)%S for d in range(1,S)],S),(nc,o.c,[o.partner],[1-o.c],2))
    for b_ in range(4):
        @pl.when(p==sqp[b_])
        def _(b=b_):
            if b==0: t=jnp.broadcast_to(jnp.sum(jnp.sum(sq[...],0,keepdims=True),1,keepdims=True),(8,128))
            else:
                buf,_,peers,at,k=hops[b-1]
                for d in sums(buf,at,peers,b-1): d.wait()
                t=total(buf,k)
            if b<3:
                buf,mine,peers,_,_=hops[b]
                nsend[b]=t; buf[mine]=t
                for d in sums(buf,[mine]*len(peers),peers,b): d.start()
            else: f_ref[...]=jnp.minimum(1.0,0.5*lax.rsqrt(t*(1.0/count)+1e-30))
    rest(p,1)
    @pl.when(j==pl.num_programs(0)-1)
    def _():
        for k in range(nf): give(k).wait()
def k3(a0T,dh,gate,up,wd,ss,left,Q1,n,L,count,points,ft=256,rc=512,nl=6,ns=4,nleft=2):
    D,T=a0T.shape; F=gate.shape[1]; z=Shards(n,D,F,ft); nf=z.nf; S=z.side
    rs,ag,lp,sqp=points; steps=max(max(t[-1] for t in rs+ag+lp),sqp[-1])//2+1
    assert len(lp)==nleft
    check_points(rs,nl,ns,1); check_gather(ag,[t[3] for t in rs]); check_gather(lp)
    cl=lambda j:jnp.minimum(j,nf-1); all_=lambda *s:pl.BlockSpec(s,lambda j:(0,)*len(s))
    col=lambda r:pl.BlockSpec((r,ft),lambda j:(0,cl(j)))
    return pl.pallas_call(functools.partial(k3_body,z=z,nl=nl,ns=ns,rc=rc,count=count,rs=rs,ag=ag,left=lp,sqp=sqp),grid=(steps,),
        in_specs=[ANY,VM,col(T),col(T),pl.BlockSpec((None,ft,D),lambda j:(L,cl(j),0)),VM,VM,ANY],
        out_specs=[ANY,all_(8,128),ANY],
        out_shape=[jax.ShapeDtypeStruct((nf,S,*z.blk),BF),jax.ShapeDtypeStruct((8,128),F32),jax.ShapeDtypeStruct(Q1.shape,BF)],input_output_aliases={7:2},
        scratch_shapes=[pltpu.VMEM((nf,S,*z.blk),BF),pltpu.VMEM((D,T),BF)]+[pltpu.VMEM((2,T,ft),BF)]*3+[pltpu.VMEM(z.blk,F32),pltpu.VMEM((3,8,128),F32),pltpu.VMEM((S,8,128),F32),pltpu.VMEM((S,8,128),F32),
            pltpu.VMEM((2,8,128),F32),DMA((3,S-1)),DMA((3,S-1)),DMA((nf,S-1)),DMA((nf,S-1)),DMA((nf,)),DMA,*Scatter.scratch(z,nl,ns),*(Gather.scratch(z,nleft) if nleft else [])],
        compiler_params=pltpu.CompilerParams(vmem_limit_bytes=67043328,collective_id=2,has_side_effects=True),name="k3",
        cost_estimate=pl.CostEstimate(flops=8*T*D*F,bytes_accessed=10*T*F,transcendentals=T*F))(a0T,dh,gate,up,wd,ss,left,Q1)


def points(rows):
    return [[ord(c) - ord("0") for c in row] for row in rows.split(",")]


K2_POINTS = (points("1257,3479,569;,78;=,9:=?,;<?A,=>AG,?@EM,ACKO"), points("79=?A,9;?AE,;=AGK,=?EMQ,?AIMQ"))
K3_POINTS = (points("359<,57;>,79=@,9;?B,;=AI,=?GS,?AMY,AEQ[,CKW_"), points("<?,>A,@I,BO,IU,S],Ya,[c,_g"), points("0369;,048;=,04:=?,06<?A"), points("_eik")[0])

def adam_body(f_ref,*refs,z,plan,ng,alias,sub,depth):
    gs,refs=refs[:ng],refs[ng:]; ins=refs[:9]; outs=refs[9+alias:18+alias]
    gb,refs=refs[18+alias],refs[19+alias:]; ib,ob,(isem,osem)=refs[:9],refs[9:18],refs[18:]
    S,ft,rg,rd,nf=z.side,z.ft,z.rg,z.rd,z.nf; rs=S//sub; hf=2*S; N=len(plan)*sub
    f=f_ref[0:1,0:1]; o=Place(S)
    places=[(l*2+h)*S+part if h is not None else o.place(l,*part) for l,h,part,_ in plan]
    def at(ref,q,t):
        p=sum(jnp.where(t//sub==k,place,0) for k,place in enumerate(places)); h=lax.rem(t,sub)
        if q%3<2: return ref.at[p,pl.ds(pl.multiple_of(h*(rs*rg),8),rs*rg)]
        return ref.at[p//hf,:,lax.rem(p,hf),pl.ds(pl.multiple_of(h*(rs*rd),8),rs*rd)]
    def reads(t):
        b=lax.rem(t,depth); return [pltpu.make_async_copy(at(ins[q],q,t),ib[q].at[b],isem.at[b,q]) for q in range(9)]
    def writes(t):
        b=lax.rem(t,depth); return [pltpu.make_async_copy(ob[q].at[b],at(outs[q],q,t),osem.at[b,q]) for q in range(9)]
    def gread(ref,part,t):
        b=lax.rem(t,depth); h=lax.rem(t,sub)
        src=(ref if part is None else ref.at[part[0],:,part[1]]).at[:,pl.ds(h*rs,rs)]
        return pltpu.make_async_copy(src,gb.at[b],isem.at[b,9])
    def fetch(t):
        for c in reads(t): c.start()
        for k,(_,h,part,a) in enumerate(plan):
            @pl.when(t//sub==k)
            def _(a=a,part=None if h is None else (h,part)): gread(gs[a],part,t).start()
    def one(g,w,m,v,wo,mo,vo,at):
        g=g.astype(F32)*f
        m=0.9*m[at]+0.1*g
        v=0.95*v[at]+0.05*g*g
        w=w[at].astype(F32)
        wo[at]=(w-0.02*(m*lax.rsqrt(v+1e-8)+0.1*w)).astype(BF); mo[at]=m; vo[at]=v
    for t in range(depth-1): fetch(jnp.int32(t))
    def unit(t,_):
        b=lax.rem(t,depth)
        @pl.when(t+depth-1<N)
        def _(): fetch(t+depth-1)
        for c in reads(t): c.wait()
        pltpu.make_async_copy(gb.at[b],gb.at[b],isem.at[b,9]).wait()
        @pl.when(t>=depth)
        def _():
            for c in writes(t-depth): c.wait()
        def tile(k,_):
            for r in range(rs):
                for q in range(3):
                    rows,cols=(rd,z.D) if q==2 else (rg,ft)
                    for c in range(0,cols,LANES):
                        g=gb[b,k,r,pl.ds(q*z.part+c//LANES*rows,rows),:]
                        at=(k,pl.ds(r*rows,rows),pl.ds(c,LANES)) if q==2 else (pl.ds(r*rows,rows),pl.ds(pl.multiple_of(k*ft+c,LANES),LANES))
                        one(g,*(ib[q+3*t_].at[b] for t_ in range(3)),*(ob[q+3*t_].at[b] for t_ in range(3)),at)
            return 0
        lax.fori_loop(0,nf,tile,0)
        for c in writes(t): c.start()
        return 0
    lax.fori_loop(0,N,unit,0)
    for t in range(max(N-depth,0),N):
        for c in writes(jnp.int32(t)): c.wait()
def adam(f,gs,plan,state,before,n,ft=256,sub=2,depth=3):
    S=round((n//2)**0.5); rows,F=state[0].shape[1:]; z=Shards(n,rows*2*S,F,ft); nf=z.nf; D=z.D
    rs=S//sub; alias=len(before); k=1+len(gs)+9; el=len(plan)*3*rows*F
    buf=lambda a,q:pltpu.VMEM((depth,rs*z.rg,F) if q%3<2 else (depth,nf,rs*z.rd,D),a.dtype)
    return pl.pallas_call(functools.partial(adam_body,z=z,plan=plan,ng=len(gs),alias=alias,sub=sub,depth=depth),
        in_specs=[VM]+[ANY]*(len(gs)+9+alias),out_specs=[ANY]*9,
        scratch_shapes=[pltpu.VMEM((depth,nf,rs,*z.blk),BF)]+[buf(a,q) for q,a in enumerate(state)]*2+[DMA((depth,10)),DMA((depth,9))],
        out_shape=[jax.ShapeDtypeStruct(a.shape,a.dtype) for a in state],input_output_aliases={k+q:q for q in range(alias)},
        compiler_params=pltpu.CompilerParams(vmem_limit_bytes=67043328),name="adamw",
        cost_estimate=pl.CostEstimate(flops=20*el,bytes_accessed=22*el,transcendentals=el))(f,*gs,*state,*before)

def solution(mesh):
    n=mesh.shape["dp"]; S=round((n//2)**0.5); hf=2*S
    at=lambda x,y,c:(x%S*S+y%S)*2+c
    def turn(d):
        return [(at(x,y,c),at(x+d*(1-c),y+d*c,c)) for x in range(S) for y in range(S) for c in range(2)]
    swap=[(i,i^1) for i in range(n)]
    def step(x,dy,*arrays):
        w,m,v=(arrays[i:i+3] for i in (0,3,6))
        L,D,F=w[0].shape; count=sum(a.size for a in w); nf=F//256; nleft=nf-len(K2_POINTS[1])
        gate,up,h1,a1,a0T=k1(x[0],*w)
        G1,ss,left,dh=k2(a1,dy[0],h1,*w,n,1,K2_POINTS)
        P,f,G1=k3(a0T,dh,gate,up,w[2],ss,left,G1,n,0,count,K3_POINTS,nleft=nleft)
        state=[a.reshape(L,nf,hf,-1,D) if k%3==2 else a.reshape(L*hf,-1,F) for k,a in enumerate((*w,*m,*v))]
        move=lambda a,p:lax.ppermute(a,"dp",p)
        near=[move(P,turn(d)) for d in range(1,S)]; theirs=move(P,swap)
        out=adam(f,[G1,P],[(1,h,q,0) for h in range(2) for q in range(S)]+[(0,None,(0,0),1)],state,[],n)
        near,theirs,out=lax.optimization_barrier((near,theirs,out))
        far=[move(a,swap) for a in near]
        out=adam(f,[theirs,*near],[(0,None,(1,0),0)]+[(0,None,(0,d),d) for d in range(1,S)],state,out,n)
        far,out=lax.optimization_barrier((far,out))
        out=adam(f,far,[(0,None,(1,d),d-1) for d in range(1,S)],state,out,n)
        return tuple(o.reshape(a.shape) for o,a in zip(out,arrays))
    P=PartitionSpec
    return jax.shard_map(step,mesh=mesh,in_specs=(P(("rep","dp"),None,None),)*2+(P(None,None,None),)*9,
        out_specs=(P("rep",None,None),)*9,check_vma=False)
```

time: 546 us -> 291 us (0.53); the launches traced: 539 us -> 290 us
  Pallas kernels: 0 us -> 286 us
  matrix products: 232 us -> 0 us
  waiting for transfers between devices: 182 us -> 0.02 us
  other arithmetic: 97.2 us -> 0 us
  between operations: 16.7 us -> 0.91 us
  local copies, waits for them, and re-layouts: 9.94 us -> 0 us
    pallas_call x0 -> x6, Pallas kernels: none -> 286 us  [the longest x1 88.2 us: k2(): pl.pallas_call(functools.partial(k2_body, z=z, nl=nl, ns=ns, rc=rc, bc=bc...]
    dot_general x15 -> x0, matrix products: 232 us -> none  [the longest x5 84.2 us: layer(): gate = jnp.dot(a, w['w_gate'], preferred_element_type=jnp.float32)]
    psum x1 -> x0, waiting for transfers between devices: 182 us -> none  [step(): summed[number] = [lax.psum(by_w[name], 'dp') for name in NAMES]]
    convert_element_type x2 -> x0, other arithmetic: 72.3 us -> none  [adamw(): return ((w - 0.02 * step).astype(jnp.bfloat16), m, v)]
    reduce_sum x4 -> x0, other arithmetic: 19.7 us -> none  [the longest x3 19 us: step(): jnp.sum(g * g)]
    unnamed x38 -> x0, local copies, waits for them, and re-layouts: 9.94 us -> none
  transfers between devices with their start and end apart: 1 -> 7, of which waited for: 1 -> 0; matrix products, arithmetic and copies ran while one was open for 0% -> 0% of each run, Pallas kernels for 0% -> 23%
where the time goes in v3:
time: 291 us; the launch traced here: 290 us
  Pallas kernels  286 us (98%)
  starting transfers between devices  3.54 us (1%)
    pallas_call x1, Pallas kernels, k2(): pl.pallas_call(functools.partial(k2_body, z=z, nl=nl, ns=ns, rc=rc, bc=bc...  88.2 us
    pallas_call x1, Pallas kernels, k3(): pl.pallas_call(functools.partial(k3_body, z=z, nl=nl, ns=ns, rc=rc, count...  84.5 us
    pallas_call x3, Pallas kernels, adam(): pl.pallas_call(functools.partial(adam_body, z=z, plan=plan, ng=len(gs), a...  81.3 us
    pallas_call x1, Pallas kernels, k1(): pl.pallas_call(functools.partial(k1_body, fc=fc), grid=(T // bm,), in_spe...  31.9 us
  transfers between devices with their start and end apart: 7, of which 0 were waited for; matrix products, arithmetic and copies ran while one was open for 0% of the time, Pallas kernels for 23%

profile of v3, /device:TPU:97, one launch (start us, length us, event | category | flops | bytes accessed | tf_op | source)
XLA Modules:
  0.0 290.4 jit_solution(14958335529114066600)
XLA Ops:
  0.6 31.9 %k1.1 = (f32[2048,2304]{1,0:T(8,128)}, f32[2048,2304]{1,0:T(8,128)}, bf16[2048,768]{1,0:T(8,128)(2,1)}, bf16[2048,768]{1,0:T(8,128)(2,1)}, bf16[768,2048]{1,0:T(8,128)(2,1)}) custom-call(bf16[2048,768]{1,0:T(8,128)(2,1)} %bitcast.56, bf16[2,768,2304]{2,1,0:T(8,128)(2,1)} %wg_h.1, bf16[2,768,2304]{2,1,0:T(8,128)(2,1)} %wu_h.1, bf16[2,2304,768]{2,1,0:T(8,128)(2,1)} %wd_ref.1), custom_call_target="tpu_custom_call" | custom-call | flops 21743271936 | bytes 47185920 | tf_op jit(solution)/shard_map/k1/pallas_call | solution.py:32
  32.5 88.2 %k2.1 = (bf16[2,9,4,4,144,128]{5,4,3,2,1,0:T(8,128)(2,1)}, f32[144,128]{1,0:T(8,128)}, bf16[4,144,128]{2,1,0:T(8,128)(2,1)}, bf16[2048,768]{1,0:T(8,128)(2,1)}) custom-call(bf16[2048,768]{1,0:T(8,128)(2,1)} %get-tuple-element.74.a_ref, bf16[2048,768]{1,0:T(8,128)(2,1)} %bitcast.57, bf16[2048,768]{1,0:T(8,128)(2,1)} %get-tuple-element.75.h_ref, ...), custom_call_target="tpu_custom_call" | custom-call | flops 57982058496 | bytes 31457280 | tf_op jit(solution)/shard_map/k2/pallas_call | solution.py:214
  120.8 84.5 %k3.1 = (bf16[9,4,144,128]{3,2,1,0:T(8,128)(2,1)}, f32[8,128]{1,0:T(8,128)}, bf16[2,9,4,4,144,128]{5,4,3,2,1,0:T(8,128)(2,1)}) custom-call(bf16[768,2048]{1,0:T(8,128)(2,1)} %get-tuple-element.73.aT_h, bf16[2048,768]{1,0:T(8,128)(2,1)} %get-tuple-element.76.dh_ref, f32[2048,2304]{1,0:T(8,128)} %get-tuple-element.77.g_ref, ...), custom_call_target="tpu_custom_call", output_to_operand_aliasing={{2}: (7, {})} | custom-call | flops 28991029248 | bytes 47185920 | tf_op jit(solution)/shard_map/k3/pallas_call | solution.py:306
  205.3 0.3 collective-permute-start.3
  205.6 0.5 collective-permute-start.2
  206.1 1.8 collective-permute-start.1
  207.8 0.0 collective-permute-start
  207.8 44.6 %adamw.3 = (bf16[16,96,2304]{2,1,0:T(8,128)(2,1)}, bf16[16,96,2304]{2,1,0:T(8,128)(2,1)}, bf16[2,9,8,32,768]{4,3,2,1,0:T(8,128)(2,1)}, f32[16,96,2304]{2,1,0:T(8...) custom-call(f32[8,128]{1,0:T(8,128)} %get-tuple-element.82.f_ref, ...), custom_call_target="tpu_custom_call" | custom-call | flops 119439360 | bytes 131383296 | tf_op jit(solution)/shard_map/adamw/pallas_call | solution.py:381
  252.5 0.0 collective-permute-done.3.refs_0_
  252.5 0.0 collective-permute-done.2.refs_3_
  252.5 0.0 collective-permute-done.1.refs_2_
  252.5 0.0 collective-permute-done.refs_1_
  252.5 0.5 collective-permute-start.4
  253.0 0.1 collective-permute-start.5
  253.1 0.4 collective-permute-start.6
  253.5 21.1 %adamw.4 = (bf16[16,96,2304]{2,1,0:T(8,128)(2,1)}, bf16[16,96,2304]{2,1,0:T(8,128)(2,1)}, bf16[2,9,8,32,768]{4,3,2,1,0:T(8,128)(2,1)}, f32[16,96,2304]{2,1,0:T(8...) custom-call(f32[8,128]{1,0:T(8,128)} %get-tuple-element.82.f_ref, ...), custom_call_target="tpu_custom_call", output_to_operand_aliasing={{0}: (14, {}), {1}: (15, {}), {2}: (16, {}), {3}: (17, {}),... | custom-call | flops 53084160 | bytes 58392576 | tf_op jit(solution)/shard_map/adamw/pallas_call | solution.py:381
  274.6 0.0 collective-permute-done.4.refs_0_
  274.6 0.0 collective-permute-done.5.refs_1_
  274.6 0.0 collective-permute-done.6.refs_2_
  274.6 15.6 %adamw.5 = (bf16[16,96,2304]{2,1,0:T(8,128)(2,1)}, bf16[16,96,2304]{2,1,0:T(8,128)(2,1)}, bf16[2,9,8,32,768]{4,3,2,1,0:T(8,128)(2,1)}, f32[16,96,2304]{2,1,0:T(8...) custom-call(f32[8,128]{1,0:T(8,128)} %get-tuple-element.82.f_ref, ...), custom_call_target="tpu_custom_call", output_to_operand_aliasing={{0}: (13, {}), {1}: (14, {}), {2}: (15, {}), {3}: (16, {}),... | custom-call | flops 39813120 | bytes 43794432 | tf_op jit(solution)/shard_map/adamw/pallas_call | solution.py:381
Async XLA Ops:
  205.3 47.2 %collective-permute-start.3 = (bf16[9,4,144,128]{3,2,1,0:T(8,128)(2,1)}, bf16[9,4,144,128]{3,2,1,0:T(8,128)(2,1)}, u32[]{:S(2)}, u32[]{:S(2)}) collective-permute-start(bf16[9,4,144,128]{3,2,1,0:T(8,128)(2,1)} %get-tuple-element.83.refs_1_), channel_id=1, source_target_pairs={{0,1},{1,0},{2,3},{3,2},{4,5},{5,4},{6,7},{7,6},{8,9},{9,8},{10,11... | collective-permute-start | bytes 3981320 | tf_op jit(solution)/shard_map/ppermute | solution.py:401
  205.6 46.9 %collective-permute-start.2 = (bf16[9,4,144,128]{3,2,1,0:T(8,128)(2,1)}, bf16[9,4,144,128]{3,2,1,0:T(8,128)(2,1)}, u32[]{:S(2)}, u32[]{:S(2)}) collective-permute-start(bf16[9,4,144,128]{3,2,1,0:T(8,128)(2,1)} %get-tuple-element.83.refs_1_), channel_id=1, source_target_pairs={{0,24},{1,7},{2,26},{3,1},{4,28},{5,3},{6,30},{7,5},{8,0},{9,15},{... | collective-permute-start | bytes 3981320 | tf_op jit(solution)/shard_map/ppermute | solution.py:401
  206.1 46.4 %collective-permute-start.1 = (bf16[9,4,144,128]{3,2,1,0:T(8,128)(2,1)}, bf16[9,4,144,128]{3,2,1,0:T(8,128)(2,1)}, u32[]{:S(2)}, u32[]{:S(2)}) collective-permute-start(bf16[9,4,144,128]{3,2,1,0:T(8,128)(2,1)} %get-tuple-element.83.refs_1_), channel_id=1, source_target_pairs={{0,16},{1,5},{2,18},{3,7},{4,20},{5,1},{6,22},{7,3},{8,24},{9,13},... | collective-permute-start | bytes 3981320 | tf_op jit(solution)/shard_map/ppermute | solution.py:401
  207.8 44.7 %collective-permute-start = (bf16[9,4,144,128]{3,2,1,0:T(8,128)(2,1)}, bf16[9,4,144,128]{3,2,1,0:T(8,128)(2,1)}, u32[]{:S(2)}, u32[]{:S(2)}) collective-permute-start(bf16[9,4,144,128]{3,2,1,0:T(8,128)(2,1)} %get-tuple-element.83.refs_1_), channel_id=1, source_target_pairs={{0,8},{1,3},{2,10},{3,5},{4,12},{5,7},{6,14},{7,1},{8,16},{9,11},{... | collective-permute-start | bytes 3981320 | tf_op jit(solution)/shard_map/ppermute | solution.py:401
  252.5 22.1 %collective-permute-start.4 = (bf16[9,4,144,128]{3,2,1,0:T(8,128)(2,1)}, bf16[9,4,144,128]{3,2,1,0:T(8,128)(2,1)}, u32[]{:S(2)}, u32[]{:S(2)}) collective-permute-start(bf16[9,4,144,128]{3,2,1,0:T(8,128)(2,1)} %collective-permute-done.refs_1_), channel_id=1, source_target_pairs={{0,1},{1,0},{2,3},{3,2},{4,5},{5,4},{6,7},{7,6},{8,9},{9,8},{10,11... | collective-permute-start | bytes 3981320 | tf_op jit(solution)/shard_map/ppermute | solution.py:401
  253.0 21.6 %collective-permute-start.5 = (bf16[9,4,144,128]{3,2,1,0:T(8,128)(2,1)}, bf16[9,4,144,128]{3,2,1,0:T(8,128)(2,1)}, u32[]{:S(2)}, u32[]{:S(2)}) collective-permute-start(bf16[9,4,144,128]{3,2,1,0:T(8,128)(2,1)} %collective-permute-done.1.refs_2_), channel_id=1, source_target_pairs={{0,1},{1,0},{2,3},{3,2},{4,5},{5,4},{6,7},{7,6},{8,9},{9,8},{10,11... | collective-permute-start | bytes 3981320 | tf_op jit(solution)/shard_map/ppermute | solution.py:401
  253.1 21.5 %collective-permute-start.6 = (bf16[9,4,144,128]{3,2,1,0:T(8,128)(2,1)}, bf16[9,4,144,128]{3,2,1,0:T(8,128)(2,1)}, u32[]{:S(2)}, u32[]{:S(2)}) collective-permute-start(bf16[9,4,144,128]{3,2,1,0:T(8,128)(2,1)} %collective-permute-done.2.refs_3_), channel_id=1, source_target_pairs={{0,1},{1,0},{2,3},{3,2},{4,5},{5,4},{6,7},{7,6},{8,9},{9,8},{10,11... | collective-permute-start | bytes 3981320 | tf_op jit(solution)/shard_map/ppermute | solution.py:401

commit v4 on v3

--- a/solution.py
+++ b/solution.py
@@ -15,25 +15,49 @@
     wide=h.astype(F32); return (wide*norm_scale(wide)).astype(BF)
 def sigmoid(g): return 0.5*jnp.tanh(0.5*g)+0.5
 
-def k1_body(x_ref,wg,wu,wd,gate_ref,up_ref,h_ref,a_ref,aT_ref,act,*,fc):
-    x=x_ref[...]; a=normed(x); F=wg.shape[1]; aT_ref[...]=a.T
-    for c in range(F//fc):
-        s=pl.ds(c*fc,fc)
-        g=dot(a,wg[:,s]); u=dot(a,wu[:,s])
-        gate_ref[:,s]=g; up_ref[:,s]=u
-        act[:,s]=(g*sigmoid(g)*u).astype(BF)
-    d=dot(act[...],wd[...]).astype(BF)
-    h=(x.astype(F32)+d.astype(F32)).astype(BF)
-    h_ref[...]=h; a_ref[...]=normed(h)
-def k1(x,wg,wu,wd,bm=512,fc=768):
+def k1_body(x_ref,wg_h,wu_h,wd_h,gate_h,up_h,h_ref,a_ref,aT_ref,wg,wu,wd,gate,up,act,wsem,osem,*,fc,L):
+    i=pl.program_id(0); bm=x_ref.shape[0]; nc=wg.shape[1]//fc; last=pl.num_programs(0)-1
+    cols=[pl.ds(c*fc,fc) for c in range(nc)]; copy=pltpu.make_async_copy
+    loads=[[copy(h.at[L,:,s],w.at[:,s],wsem.at[q,c]) for q,(h,w) in enumerate(((wg_h,wg),(wu_h,wu)))] for c,s in enumerate(cols)]
+    down=copy(wd_h.at[L],wd,wsem.at[2,0])
+    stores=lambda t:[[copy(b.at[c],h.at[pl.ds(pl.multiple_of(t*bm,bm),bm),s],osem.at[q,c]) for q,(b,h) in enumerate(((gate,gate_h),(up,up_h)))] for c,s in enumerate(cols)]
+    def work(first):
+        x=x_ref[...]; a=normed(x)
+        for c,s in enumerate(cols):
+            if first:
+                for w in loads[c]: w.wait()
+            g=dot(a,wg[:,s]); u=dot(a,wu[:,s])
+            gate[c]=g; up[c]=u
+            act[:,s]=(g*sigmoid(g)*u).astype(BF)
+            for w in stores(i)[c]: w.start()
+        aT_ref[...]=a.T
+        if first: down.wait()
+        d=dot(act[...],wd[...]).astype(BF)
+        h=(x.astype(F32)+d.astype(F32)).astype(BF)
+        h_ref[...]=h; a_ref[...]=normed(h)
+    @pl.when(i==0)
+    def _():
+        for c in range(nc):
+            for w in loads[c]: w.start()
+        down.start()
+        work(True)
+    @pl.when(i>0)
+    def _():
+        for c in stores(i-1):
+            for w in c: w.wait()
+        work(False)
+    @pl.when(i==last)
+    def _():
+        for c in stores(i):
+            for w in c: w.wait()
+def k1(x,wg,wu,wd,L=0,bm=512,fc=768):
     T,D=x.shape; F=wg.shape[2]
-    wspec=lambda r,c:pl.BlockSpec((None,r,c),lambda i:(0,0,0),pipeline_mode=pl.Buffered(1))
     row=lambda c:pl.BlockSpec((bm,c),lambda i:(i,0))
-    return pl.pallas_call(functools.partial(k1_body,fc=fc),grid=(T//bm,),
-        in_specs=[row(D),wspec(D,F),wspec(D,F),wspec(F,D)],
-        out_specs=[row(F),row(F),row(D),row(D),pl.BlockSpec((D,bm),lambda i:(0,i))],
+    return pl.pallas_call(functools.partial(k1_body,fc=fc,L=L),grid=(T//bm,),
+        in_specs=[row(D),ANY,ANY,ANY],out_specs=[ANY,ANY,row(D),row(D),pl.BlockSpec((D,bm),lambda i:(0,i))],
         out_shape=[jax.ShapeDtypeStruct((T,F),F32)]*2+[jax.ShapeDtypeStruct((T,D),BF)]*2+[jax.ShapeDtypeStruct((D,T),BF)],
-        scratch_shapes=[pltpu.VMEM((bm,F),BF)],
+        scratch_shapes=[pltpu.VMEM((D,F),BF),pltpu.VMEM((D,F),BF),pltpu.VMEM((F,D),BF),pltpu.VMEM((F//fc,bm,fc),F32),pltpu.VMEM((F//fc,bm,fc),F32),
+            pltpu.VMEM((bm,F),BF),pltpu.SemaphoreType.DMA((3,F//fc)),pltpu.SemaphoreType.DMA((2,F//fc))],
         compiler_params=pltpu.CompilerParams(vmem_limit_bytes=60<<20),name="k1",
         cost_estimate=pl.CostEstimate(flops=6*T*D*F,bytes_accessed=10*T*F,transcendentals=T*F))(x,wg,wu,wd)
 
@@ -219,10 +243,11 @@
         compiler_params=pltpu.CompilerParams(vmem_limit_bytes=67043328,collective_id=1,has_side_effects=True),name="k2",
         cost_estimate=pl.CostEstimate(flops=16*T*D*F,bytes_accessed=30<<20,transcendentals=T*F))(a1,dy,h1,wg,wu,wd)
 
-def k3_body(aT_h,dh_ref,g_ref,u_ref,wd_ref,ss_ref,left_ref,Q1_,P_out,f_ref,Q1,P_ref,aT,dg,du,act,sq,nsend,nv,nu,nc,nS,nR,gS,gR,oS,sem,*refs,z,nl,ns,rc,count,rs,ag,left,sqp):
+def k3_body(aT_h,dh_ref,g_ref,u_ref,wd_ref,ss_ref,left_ref,Q1_,P_out,f_ref,Q1,P_ref,aT,dg,du,act,sq,nsend,nplane,nc,nS,nR,gS,gR,oS,sem,*refs,z,nl,ns,rc,count,rs,ag,left,sqp):
     j=pl.program_id(0); D,T=aT.shape; nf,S=z.nf,z.side
     o=Place(S); sc=Scatter(z,o,nl,ns,refs[:Scatter.N])
     nleft=len(left); gl=Gather(z,o,nf-nleft,Q1,refs[Scatter.N:]) if nleft else None
+    apart=[(a,b) for a in range(S) for b in range(S) if a or b]; plane=[o.dev(o.u+a,o.v+b) for a,b in apart]
     to=lambda k,here=False:[send(P_ref.at[k,o.v],P_ref.at[k,(o.v+S-d)%S if here else o.v],gS.at[k,d-1],gR.at[k,d-1],o.vpeer[d-1]) for d in range(1,S)]
     def done(k,g):
         w=g.astype(F32); sq[...]+=w*w
@@ -251,7 +276,7 @@
     @pl.when(j==0)
     def _():
         load.start()
-        o.greet((o.partner,*o.upeer,*o.vpeer))
+        o.greet((o.partner,*plane))
         sq[...]=ss_ref[...]
         for k in range(nleft): gl.P[k,o.v]=left_ref[k]
         front(rows[:half],b)
@@ -261,7 +286,7 @@
     @pl.when(j==nf)
     def _(): back(j-1,0,1-b)
     @pl.when(j==0)
-    def _(): pl.semaphore_wait(pltpu.get_barrier_semaphore(),1+len(o.upeer)+len(o.vpeer))
+    def _(): pl.semaphore_wait(pltpu.get_barrier_semaphore(),1+len(plane))
     reduce_(2*j,0); rest(2*j,0)
     @pl.when(j==0)
     def _():
@@ -274,20 +299,17 @@
     p=2*j+1
     reduce_(p,1)
     def sums(buf,at,peers,b): return [send(nsend.at[b],buf.at[a],nS.at[b,i],nR.at[b,i],d) for i,(a,d) in enumerate(zip(at,peers))]
-    def total(ref,k):
-        t=ref[0]
-        for i in range(1,k): t=t+ref[i]
-        return t
-    hops=((nv,o.v,o.vpeer,[(o.v+S-d)%S for d in range(1,S)],S),(nu,o.u,o.upeer,[(o.u+S-d)%S for d in range(1,S)],S),(nc,o.c,[o.partner],[1-o.c],2))
-    for b_ in range(4):
+    hops=((nplane,o.u*S+o.v,plane,[(o.u+S-a)%S*S+(o.v+S-b)%S for a,b in apart],S*S),(nc,o.c,[o.partner],[1-o.c],2))
+    for b_ in range(3):
         @pl.when(p==sqp[b_])
         def _(b=b_):
             if b==0: t=jnp.broadcast_to(jnp.sum(jnp.sum(sq[...],0,keepdims=True),1,keepdims=True),(8,128))
             else:
                 buf,_,peers,at,k=hops[b-1]
                 for d in sums(buf,at,peers,b-1): d.wait()
-                t=total(buf,k)
-            if b<3:
+                t=buf[0]
+                for i in range(1,k): t=t+buf[i]
+            if b<2:
                 buf,mine,peers,_,_=hops[b]
                 nsend[b]=t; buf[mine]=t
                 for d in sums(buf,[mine]*len(peers),peers,b): d.start()
@@ -307,8 +329,8 @@
         in_specs=[ANY,VM,col(T),col(T),pl.BlockSpec((None,ft,D),lambda j:(L,cl(j),0)),VM,VM,ANY],
         out_specs=[ANY,all_(8,128),ANY],
         out_shape=[jax.ShapeDtypeStruct((nf,S,*z.blk),BF),jax.ShapeDtypeStruct((8,128),F32),jax.ShapeDtypeStruct(Q1.shape,BF)],input_output_aliases={7:2},
-        scratch_shapes=[pltpu.VMEM((nf,S,*z.blk),BF),pltpu.VMEM((D,T),BF)]+[pltpu.VMEM((2,T,ft),BF)]*3+[pltpu.VMEM(z.blk,F32),pltpu.VMEM((3,8,128),F32),pltpu.VMEM((S,8,128),F32),pltpu.VMEM((S,8,128),F32),
-            pltpu.VMEM((2,8,128),F32),DMA((3,S-1)),DMA((3,S-1)),DMA((nf,S-1)),DMA((nf,S-1)),DMA((nf,)),DMA,*Scatter.scratch(z,nl,ns),*(Gather.scratch(z,nleft) if nleft else [])],
+        scratch_shapes=[pltpu.VMEM((nf,S,*z.blk),BF),pltpu.VMEM((D,T),BF)]+[pltpu.VMEM((2,T,ft),BF)]*3+[pltpu.VMEM(z.blk,F32),pltpu.VMEM((2,8,128),F32),pltpu.VMEM((S*S,8,128),F32),
+            pltpu.VMEM((2,8,128),F32),DMA((2,S*S)),DMA((2,S*S)),DMA((nf,S-1)),DMA((nf,S-1)),DMA((nf,)),DMA,*Scatter.scratch(z,nl,ns),*(Gather.scratch(z,nleft) if nleft else [])],
         compiler_params=pltpu.CompilerParams(vmem_limit_bytes=67043328,collective_id=2,has_side_effects=True),name="k3",
         cost_estimate=pl.CostEstimate(flops=8*T*D*F,bytes_accessed=10*T*F,transcendentals=T*F))(a0T,dh,gate,up,wd,ss,left,Q1)
 
@@ -317,8 +339,8 @@
     return [[ord(c) - ord("0") for c in row] for row in rows.split(",")]
 
 
-K2_POINTS = (points("1257,3479,569;,78;=,9:=?,;<?A,=>AG,?@EM,ACKO"), points("79=?A,9;?AE,;=AGK,=?EMQ,?AIMQ"))
-K3_POINTS = (points("359<,57;>,79=@,9;?B,;=AI,=?GS,?AMY,AEQ[,CKW_"), points("<?,>A,@I,BO,IU,S],Ya,[c,_g"), points("0369;,048;=,04:=?,06<?A"), points("_eik")[0])
+K2_POINTS = (points("1257,3479,569;,78;=,9:=?,;<?A,=>AG,?@GM,ACKQ"), points("79=?A,9;?CG,;=AGK,=?EMQ,?AIOS"))
+K3_POINTS = (points("359<,57;>,79=A,9;?B,;<AI,=?EQ,?AKW,ACOY,CGS]"), points("<?,>A,AG,BM,IU,Q[,W_,Ya,]c"), points("036:;,047;=,047<=,048<>"), points("]eg")[0])
 
 def adam_body(f_ref,*refs,z,plan,ng,alias,sub,depth):
     gs,refs=refs[:ng],refs[ng:]; ins=refs[:9]; outs=refs[9+alias:18+alias]
@@ -374,7 +396,7 @@
     lax.fori_loop(0,N,unit,0)
     for t in range(max(N-depth,0),N):
         for c in writes(jnp.int32(t)): c.wait()
-def adam(f,gs,plan,state,before,n,ft=256,sub=2,depth=3):
+def adam(f,gs,plan,state,before,n,ft=256,sub=2,depth=4):
     S=round((n//2)**0.5); rows,F=state[0].shape[1:]; z=Shards(n,rows*2*S,F,ft); nf=z.nf; D=z.D
     rs=S//sub; alias=len(before); k=1+len(gs)+9; el=len(plan)*3*rows*F
     buf=lambda a,q:pltpu.VMEM((depth,rs*z.rg,F) if q%3<2 else (depth,nf,rs*z.rd,D),a.dtype)

time: 291 us -> 290 us (level)
  Pallas kernels: 286 us -> 283 us
    pallas_call x1, Pallas kernels: 84.5 us -> 81.4 us  [k3(): pl.pallas_call(functools.partial(k3_body, z=z, nl=nl, ns=ns, rc=rc, count...]
where the time goes in v4:
time: 290 us; the launch traced here: 289 us
  Pallas kernels  283 us (98%)
  starting transfers between devices  5.39 us (2%)
    pallas_call x1, Pallas kernels, k2(): pl.pallas_call(functools.partial(k2_body, z=z, nl=nl, ns=ns, rc=rc, bc=bc...  88.6 us
    pallas_call x3, Pallas kernels, adam(): pl.pallas_call(functools.partial(adam_body, z=z, plan=plan, ng=len(gs), a...  81.7 us
    pallas_call x1, Pallas kernels, k3(): pl.pallas_call(functools.partial(k3_body, z=z, nl=nl, ns=ns, rc=rc, count...  81.4 us
    pallas_call x1, Pallas kernels, k1(): pl.pallas_call(functools.partial(k1_body, fc=fc, L=L), grid=(T // bm,), i...  31.3 us
  transfers between devices with their start and end apart: 7, of which 0 were waited for; matrix products, arithmetic and copies ran while one was open for 0% of the time, Pallas kernels for 23%

profile of v4, /device:TPU:97, one launch (start us, length us, event | category | flops | bytes accessed | tf_op | source)
XLA Modules:
  0.0 289.4 jit_solution(11770620095542624712)
XLA Ops:
  0.6 31.3 %k1.1 = (f32[2048,2304]{1,0:T(8,128)}, f32[2048,2304]{1,0:T(8,128)}, bf16[2048,768]{1,0:T(8,128)(2,1)}, bf16[2048,768]{1,0:T(8,128)(2,1)}, bf16[768,2048]{1,0:T(8,128)(2,1)}) custom-call(bf16[2048,768]{1,0:T(8,128)(2,1)} %bitcast.56, bf16[2,768,2304]{2,1,0:T(8,128)(2,1)} %wg_h.3, bf16[2,768,2304]{2,1,0:T(8,128)(2,1)} %wu_h.3, bf16[2,2304,768]{2,1,0:T(8,128)(2,1)} %wd_ref.1), custom_call_target="tpu_custom_call" | custom-call | flops 21743271936 | bytes 47185920 | tf_op jit(solution)/shard_map/k1/pallas_call | solution.py:56
  31.9 88.6 %k2.1 = (bf16[2,9,4,4,144,128]{5,4,3,2,1,0:T(8,128)(2,1)}, f32[144,128]{1,0:T(8,128)}, bf16[4,144,128]{2,1,0:T(8,128)(2,1)}, bf16[2048,768]{1,0:T(8,128)(2,1)}) custom-call(bf16[2048,768]{1,0:T(8,128)(2,1)} %get-tuple-element.74.a_ref, bf16[2048,768]{1,0:T(8,128)(2,1)} %bitcast.57, bf16[2048,768]{1,0:T(8,128)(2,1)} %get-tuple-element.75.h_ref, ...), custom_call_target="tpu_custom_call" | custom-call | flops 57982058496 | bytes 31457280 | tf_op jit(solution)/shard_map/k2/pallas_call | solution.py:238
  120.5 81.4 %k3.1 = (bf16[9,4,144,128]{3,2,1,0:T(8,128)(2,1)}, f32[8,128]{1,0:T(8,128)}, bf16[2,9,4,4,144,128]{5,4,3,2,1,0:T(8,128)(2,1)}) custom-call(bf16[768,2048]{1,0:T(8,128)(2,1)} %get-tuple-element.73.aT_h, bf16[2048,768]{1,0:T(8,128)(2,1)} %get-tuple-element.76.dh_ref, f32[2048,2304]{1,0:T(8,128)} %get-tuple-element.77.g_ref, ...), custom_call_target="tpu_custom_call", output_to_operand_aliasing={{2}: (7, {})} | custom-call | flops 28991029248 | bytes 47185920 | tf_op jit(solution)/shard_map/k3/pallas_call | solution.py:328
  202.0 0.3 collective-permute-start.3
  202.2 1.1 collective-permute-start.2
  203.4 1.4 collective-permute-start.1
  204.8 0.0 collective-permute-start
  204.8 44.2 %adamw.3 = (bf16[16,96,2304]{2,1,0:T(8,128)(2,1)}, bf16[16,96,2304]{2,1,0:T(8,128)(2,1)}, bf16[2,9,8,32,768]{4,3,2,1,0:T(8,128)(2,1)}, f32[16,96,2304]{2,1,0:T(8...) custom-call(f32[8,128]{1,0:T(8,128)} %get-tuple-element.82.f_ref, ...), custom_call_target="tpu_custom_call" | custom-call | flops 119439360 | bytes 131383296 | tf_op jit(solution)/shard_map/adamw/pallas_call | solution.py:403
  249.0 0.0 collective-permute-done.3.refs_0_
  249.1 0.0 collective-permute-done.2.refs_3_
  249.1 0.0 collective-permute-done.1.refs_2_
  249.1 0.0 collective-permute-done.refs_1_
  249.1 2.1 collective-permute-start.4
  251.1 0.1 collective-permute-start.5
  251.3 0.4 collective-permute-start.6
  251.7 21.4 %adamw.4 = (bf16[16,96,2304]{2,1,0:T(8,128)(2,1)}, bf16[16,96,2304]{2,1,0:T(8,128)(2,1)}, bf16[2,9,8,32,768]{4,3,2,1,0:T(8,128)(2,1)}, f32[16,96,2304]{2,1,0:T(8...) custom-call(f32[8,128]{1,0:T(8,128)} %get-tuple-element.82.f_ref, ...), custom_call_target="tpu_custom_call", output_to_operand_aliasing={{0}: (14, {}), {1}: (15, {}), {2}: (16, {}), {3}: (17, {}),... | custom-call | flops 53084160 | bytes 58392576 | tf_op jit(solution)/shard_map/adamw/pallas_call | solution.py:403
  273.0 0.0 collective-permute-done.4.refs_0_
  273.0 0.0 collective-permute-done.5.refs_1_
  273.0 0.0 collective-permute-done.6.refs_2_
  273.1 16.1 %adamw.5 = (bf16[16,96,2304]{2,1,0:T(8,128)(2,1)}, bf16[16,96,2304]{2,1,0:T(8,128)(2,1)}, bf16[2,9,8,32,768]{4,3,2,1,0:T(8,128)(2,1)}, f32[16,96,2304]{2,1,0:T(8...) custom-call(f32[8,128]{1,0:T(8,128)} %get-tuple-element.82.f_ref, ...), custom_call_target="tpu_custom_call", output_to_operand_aliasing={{0}: (13, {}), {1}: (14, {}), {2}: (15, {}), {3}: (16, {}),... | custom-call | flops 39813120 | bytes 43794432 | tf_op jit(solution)/shard_map/adamw/pallas_call | solution.py:403
Async XLA Ops:
  202.0 47.1 %collective-permute-start.3 = (bf16[9,4,144,128]{3,2,1,0:T(8,128)(2,1)}, bf16[9,4,144,128]{3,2,1,0:T(8,128)(2,1)}, u32[]{:S(2)}, u32[]{:S(2)}) collective-permute-start(bf16[9,4,144,128]{3,2,1,0:T(8,128)(2,1)} %get-tuple-element.83.refs_1_), channel_id=1, source_target_pairs={{0,1},{1,0},{2,3},{3,2},{4,5},{5,4},{6,7},{7,6},{8,9},{9,8},{10,11... | collective-permute-start | bytes 3981320 | tf_op jit(solution)/shard_map/ppermute | solution.py:423
  202.2 46.8 %collective-permute-start.2 = (bf16[9,4,144,128]{3,2,1,0:T(8,128)(2,1)}, bf16[9,4,144,128]{3,2,1,0:T(8,128)(2,1)}, u32[]{:S(2)}, u32[]{:S(2)}) collective-permute-start(bf16[9,4,144,128]{3,2,1,0:T(8,128)(2,1)} %get-tuple-element.83.refs_1_), channel_id=1, source_target_pairs={{0,24},{1,7},{2,26},{3,1},{4,28},{5,3},{6,30},{7,5},{8,0},{9,15},{... | collective-permute-start | bytes 3981320 | tf_op jit(solution)/shard_map/ppermute | solution.py:423
  203.4 45.7 %collective-permute-start.1 = (bf16[9,4,144,128]{3,2,1,0:T(8,128)(2,1)}, bf16[9,4,144,128]{3,2,1,0:T(8,128)(2,1)}, u32[]{:S(2)}, u32[]{:S(2)}) collective-permute-start(bf16[9,4,144,128]{3,2,1,0:T(8,128)(2,1)} %get-tuple-element.83.refs_1_), channel_id=1, source_target_pairs={{0,16},{1,5},{2,18},{3,7},{4,20},{5,1},{6,22},{7,3},{8,24},{9,13},... | collective-permute-start | bytes 3981320 | tf_op jit(solution)/shard_map/ppermute | solution.py:423
  204.8 44.3 %collective-permute-start = (bf16[9,4,144,128]{3,2,1,0:T(8,128)(2,1)}, bf16[9,4,144,128]{3,2,1,0:T(8,128)(2,1)}, u32[]{:S(2)}, u32[]{:S(2)}) collective-permute-start(bf16[9,4,144,128]{3,2,1,0:T(8,128)(2,1)} %get-tuple-element.83.refs_1_), channel_id=1, source_target_pairs={{0,8},{1,3},{2,10},{3,5},{4,12},{5,7},{6,14},{7,1},{8,16},{9,11},{... | collective-permute-start | bytes 3981320 | tf_op jit(solution)/shard_map/ppermute | solution.py:423
  249.1 23.9 %collective-permute-start.4 = (bf16[9,4,144,128]{3,2,1,0:T(8,128)(2,1)}, bf16[9,4,144,128]{3,2,1,0:T(8,128)(2,1)}, u32[]{:S(2)}, u32[]{:S(2)}) collective-permute-start(bf16[9,4,144,128]{3,2,1,0:T(8,128)(2,1)} %collective-permute-done.refs_1_), channel_id=1, source_target_pairs={{0,1},{1,0},{2,3},{3,2},{4,5},{5,4},{6,7},{7,6},{8,9},{9,8},{10,11... | collective-permute-start | bytes 3981320 | tf_op jit(solution)/shard_map/ppermute | solution.py:423
  251.1 21.9 %collective-permute-start.5 = (bf16[9,4,144,128]{3,2,1,0:T(8,128)(2,1)}, bf16[9,4,144,128]{3,2,1,0:T(8,128)(2,1)}, u32[]{:S(2)}, u32[]{:S(2)}) collective-permute-start(bf16[9,4,144,128]{3,2,1,0:T(8,128)(2,1)} %collective-permute-done.1.refs_2_), channel_id=1, source_target_pairs={{0,1},{1,0},{2,3},{3,2},{4,5},{5,4},{6,7},{7,6},{8,9},{9,8},{10,11... | collective-permute-start | bytes 3981320 | tf_op jit(solution)/shard_map/ppermute | solution.py:423
  251.3 21.8 %collective-permute-start.6 = (bf16[9,4,144,128]{3,2,1,0:T(8,128)(2,1)}, bf16[9,4,144,128]{3,2,1,0:T(8,128)(2,1)}, u32[]{:S(2)}, u32[]{:S(2)}) collective-permute-start(bf16[9,4,144,128]{3,2,1,0:T(8,128)(2,1)} %collective-permute-done.2.refs_3_), channel_id=1, source_target_pairs={{0,1},{1,0},{2,3},{3,2},{4,5},{5,4},{6,7},{7,6},{8,9},{9,8},{10,11... | collective-permute-start | bytes 3981320 | tf_op jit(solution)/shard_map/ppermute | solution.py:423

commit v5 on v3

--- a/solution.py
+++ b/solution.py
@@ -219,14 +219,16 @@
         compiler_params=pltpu.CompilerParams(vmem_limit_bytes=67043328,collective_id=1,has_side_effects=True),name="k2",
         cost_estimate=pl.CostEstimate(flops=16*T*D*F,bytes_accessed=30<<20,transcendentals=T*F))(a1,dy,h1,wg,wu,wd)
 
-def k3_body(aT_h,dh_ref,g_ref,u_ref,wd_ref,ss_ref,left_ref,Q1_,P_out,f_ref,Q1,P_ref,aT,dg,du,act,sq,nsend,nv,nu,nc,nS,nR,gS,gR,oS,sem,*refs,z,nl,ns,rc,count,rs,ag,left,sqp):
+def k3_body(aT_h,dh_ref,g_ref,u_ref,wd_ref,ss_ref,left_ref,Q1_,P_out,f_ref,Q1,P_ref,aT,dg,du,act,sq,nsend,nplane,nc,nS,nR,gS,gR,oS,sem,*refs,z,nl,ns,rc,count,rs,ag,left,sqp):
     j=pl.program_id(0); D,T=aT.shape; nf,S=z.nf,z.side
     o=Place(S); sc=Scatter(z,o,nl,ns,refs[:Scatter.N])
     nleft=len(left); gl=Gather(z,o,nf-nleft,Q1,refs[Scatter.N:]) if nleft else None
+    apart=[(a,b) for a in range(S) for b in range(S) if a or b]; plane=[o.dev(o.u+a,o.v+b) for a,b in apart]
     to=lambda k,here=False:[send(P_ref.at[k,o.v],P_ref.at[k,(o.v+S-d)%S if here else o.v],gS.at[k,d-1],gR.at[k,d-1],o.vpeer[d-1]) for d in range(1,S)]
     def done(k,g):
         w=g.astype(F32); sq[...]+=w*w
         P_ref[k,o.v]=g
+    def hand(k):
         for d in to(k): d.start()
     def there(k):
         for d in to(k,True): d.wait()
@@ -238,6 +240,7 @@
         if nleft:
             for i in (4,3,2,1,0): run([t[i] for t in left],p,parity,lambda k:gl.step(i,k))
         run([t[1] for t in ag],p,parity,there)
+        run([t[0] for t in ag],p,parity,hand)
     load=pltpu.make_async_copy(aT_h,aT,sem)
     def front(rows,b):
         for r in rows:
@@ -251,7 +254,7 @@
     @pl.when(j==0)
     def _():
         load.start()
-        o.greet((o.partner,*o.upeer,*o.vpeer))
+        o.greet((o.partner,*plane))
         sq[...]=ss_ref[...]
         for k in range(nleft): gl.P[k,o.v]=left_ref[k]
         front(rows[:half],b)
@@ -261,7 +264,7 @@
     @pl.when(j==nf)
     def _(): back(j-1,0,1-b)
     @pl.when(j==0)
-    def _(): pl.semaphore_wait(pltpu.get_barrier_semaphore(),1+len(o.upeer)+len(o.vpeer))
+    def _(): pl.semaphore_wait(pltpu.get_barrier_semaphore(),1+len(plane))
     reduce_(2*j,0); rest(2*j,0)
     @pl.when(j==0)
     def _():
@@ -274,20 +277,17 @@
     p=2*j+1
     reduce_(p,1)
     def sums(buf,at,peers,b): return [send(nsend.at[b],buf.at[a],nS.at[b,i],nR.at[b,i],d) for i,(a,d) in enumerate(zip(at,peers))]
-    def total(ref,k):
-        t=ref[0]
-        for i in range(1,k): t=t+ref[i]
-        return t
-    hops=((nv,o.v,o.vpeer,[(o.v+S-d)%S for d in range(1,S)],S),(nu,o.u,o.upeer,[(o.u+S-d)%S for d in range(1,S)],S),(nc,o.c,[o.partner],[1-o.c],2))
-    for b_ in range(4):
+    hops=((nplane,o.u*S+o.v,plane,[(o.u+S-a)%S*S+(o.v+S-b)%S for a,b in apart],S*S),(nc,o.c,[o.partner],[1-o.c],2))
+    for b_ in range(3):
         @pl.when(p==sqp[b_])
         def _(b=b_):
             if b==0: t=jnp.broadcast_to(jnp.sum(jnp.sum(sq[...],0,keepdims=True),1,keepdims=True),(8,128))
             else:
                 buf,_,peers,at,k=hops[b-1]
                 for d in sums(buf,at,peers,b-1): d.wait()
-                t=total(buf,k)
-            if b<3:
+                t=buf[0]
+                for i in range(1,k): t=t+buf[i]
+            if b<2:
                 buf,mine,peers,_,_=hops[b]
                 nsend[b]=t; buf[mine]=t
                 for d in sums(buf,[mine]*len(peers),peers,b): d.start()
@@ -300,15 +300,15 @@
     D,T=a0T.shape; F=gate.shape[1]; z=Shards(n,D,F,ft); nf=z.nf; S=z.side
     rs,ag,lp,sqp=points; steps=max(max(t[-1] for t in rs+ag+lp),sqp[-1])//2+1
     assert len(lp)==nleft
-    check_points(rs,nl,ns,1); check_gather(ag,[t[3] for t in rs]); check_gather(lp)
+    check_points(rs,nl,ns,1); check_gather(ag); check_gather(lp); assert all(a[0]>=r[3] for a,r in zip(ag,rs))
     cl=lambda j:jnp.minimum(j,nf-1); all_=lambda *s:pl.BlockSpec(s,lambda j:(0,)*len(s))
     col=lambda r:pl.BlockSpec((r,ft),lambda j:(0,cl(j)))
     return pl.pallas_call(functools.partial(k3_body,z=z,nl=nl,ns=ns,rc=rc,count=count,rs=rs,ag=ag,left=lp,sqp=sqp),grid=(steps,),
         in_specs=[ANY,VM,col(T),col(T),pl.BlockSpec((None,ft,D),lambda j:(L,cl(j),0)),VM,VM,ANY],
         out_specs=[ANY,all_(8,128),ANY],
         out_shape=[jax.ShapeDtypeStruct((nf,S,*z.blk),BF),jax.ShapeDtypeStruct((8,128),F32),jax.ShapeDtypeStruct(Q1.shape,BF)],input_output_aliases={7:2},
-        scratch_shapes=[pltpu.VMEM((nf,S,*z.blk),BF),pltpu.VMEM((D,T),BF)]+[pltpu.VMEM((2,T,ft),BF)]*3+[pltpu.VMEM(z.blk,F32),pltpu.VMEM((3,8,128),F32),pltpu.VMEM((S,8,128),F32),pltpu.VMEM((S,8,128),F32),
-            pltpu.VMEM((2,8,128),F32),DMA((3,S-1)),DMA((3,S-1)),DMA((nf,S-1)),DMA((nf,S-1)),DMA((nf,)),DMA,*Scatter.scratch(z,nl,ns),*(Gather.scratch(z,nleft) if nleft else [])],
+        scratch_shapes=[pltpu.VMEM((nf,S,*z.blk),BF),pltpu.VMEM((D,T),BF)]+[pltpu.VMEM((2,T,ft),BF)]*3+[pltpu.VMEM(z.blk,F32),pltpu.VMEM((2,8,128),F32),pltpu.VMEM((S*S,8,128),F32),
+            pltpu.VMEM((2,8,128),F32),DMA((2,S*S)),DMA((2,S*S)),DMA((nf,S-1)),DMA((nf,S-1)),DMA((nf,)),DMA,*Scatter.scratch(z,nl,ns),*(Gather.scratch(z,nleft) if nleft else [])],
         compiler_params=pltpu.CompilerParams(vmem_limit_bytes=67043328,collective_id=2,has_side_effects=True),name="k3",
         cost_estimate=pl.CostEstimate(flops=8*T*D*F,bytes_accessed=10*T*F,transcendentals=T*F))(a0T,dh,gate,up,wd,ss,left,Q1)
 
@@ -318,7 +318,7 @@
 
 
 K2_POINTS = (points("1257,3479,569;,78;=,9:=?,;<?A,=>AG,?@EM,ACKO"), points("79=?A,9;?AE,;=AGK,=?EMQ,?AIMQ"))
-K3_POINTS = (points("359<,57;>,79=@,9;?B,;=AI,=?GS,?AMY,AEQ[,CKW_"), points("<?,>A,@I,BO,IU,S],Ya,[c,_g"), points("0369;,048;=,04:=?,06<?A"), points("_eik")[0])
+K3_POINTS = (points("35:>,57<@,79>B,9;?G,;=AI,=?EO,?AKS,ACMU,CIQW"), points("QY,QY,QY,QY,QY,QY,SY,UY,W["), points("048<>,048=?,04:>@,06;@B"), points("WY[")[0])
 
 def adam_body(f_ref,*refs,z,plan,ng,alias,sub,depth):
     gs,refs=refs[:ng],refs[ng:]; ins=refs[:9]; outs=refs[9+alias:18+alias]

time: 291 us -> 289 us (level)
  no operation moved by 1% of the time
where the time goes in v5:
time: 289 us
  Pallas kernels  284 us (98%)
  starting transfers between devices  4 us (1%)
    pallas_call x1, Pallas kernels, k2(): pl.pallas_call(functools.partial(k2_body, z=z, nl=nl, ns=ns, rc=rc, bc=bc...  88.2 us
    pallas_call x1, Pallas kernels, k3(): pl.pallas_call(functools.partial(k3_body, z=z, nl=nl, ns=ns, rc=rc, count...  82.9 us
    pallas_call x3, Pallas kernels, adam(): pl.pallas_call(functools.partial(adam_body, z=z, plan=plan, ng=len(gs), a...  81.3 us
    pallas_call x1, Pallas kernels, k1(): pl.pallas_call(functools.partial(k1_body, fc=fc), grid=(T // bm,), in_spe...  31.9 us
  transfers between devices with their start and end apart: 7, of which 0 were waited for; matrix products, arithmetic and copies ran while one was open for 0% of the time, Pallas kernels for 23%

profile of v5, /device:TPU:97, one launch (start us, length us, event | category | flops | bytes accessed | tf_op | source)
XLA Modules:
  0.0 289.2 jit_solution(11931767591780896091)
XLA Ops:
  0.6 31.9 %k1.1 = (f32[2048,2304]{1,0:T(8,128)}, f32[2048,2304]{1,0:T(8,128)}, bf16[2048,768]{1,0:T(8,128)(2,1)}, bf16[2048,768]{1,0:T(8,128)(2,1)}, bf16[768,2048]{1,0:T(8,128)(2,1)}) custom-call(bf16[2048,768]{1,0:T(8,128)(2,1)} %bitcast.56, bf16[2,768,2304]{2,1,0:T(8,128)(2,1)} %wg_h.1, bf16[2,768,2304]{2,1,0:T(8,128)(2,1)} %wu_h.1, bf16[2,2304,768]{2,1,0:T(8,128)(2,1)} %wd_ref.1), custom_call_target="tpu_custom_call" | custom-call | flops 21743271936 | bytes 47185920 | tf_op jit(solution)/shard_map/k1/pallas_call | solution.py:32
  32.5 88.2 %k2.1 = (bf16[2,9,4,4,144,128]{5,4,3,2,1,0:T(8,128)(2,1)}, f32[144,128]{1,0:T(8,128)}, bf16[4,144,128]{2,1,0:T(8,128)(2,1)}, bf16[2048,768]{1,0:T(8,128)(2,1)}) custom-call(bf16[2048,768]{1,0:T(8,128)(2,1)} %get-tuple-element.74.a_ref, bf16[2048,768]{1,0:T(8,128)(2,1)} %bitcast.57, bf16[2048,768]{1,0:T(8,128)(2,1)} %get-tuple-element.75.h_ref, ...), custom_call_target="tpu_custom_call" | custom-call | flops 57982058496 | bytes 31457280 | tf_op jit(solution)/shard_map/k2/pallas_call | solution.py:214
  120.8 82.9 %k3.1 = (bf16[9,4,144,128]{3,2,1,0:T(8,128)(2,1)}, f32[8,128]{1,0:T(8,128)}, bf16[2,9,4,4,144,128]{5,4,3,2,1,0:T(8,128)(2,1)}) custom-call(bf16[768,2048]{1,0:T(8,128)(2,1)} %get-tuple-element.73.aT_h, bf16[2048,768]{1,0:T(8,128)(2,1)} %get-tuple-element.76.dh_ref, f32[2048,2304]{1,0:T(8,128)} %get-tuple-element.77.g_ref, ...), custom_call_target="tpu_custom_call", output_to_operand_aliasing={{2}: (7, {})} | custom-call | flops 28991029248 | bytes 47185920 | tf_op jit(solution)/shard_map/k3/pallas_call | solution.py:306
  203.6 0.3 collective-permute-start.3
  203.9 2.4 collective-permute-start.2
  206.3 0.0 collective-permute-start.1
  206.3 0.6 collective-permute-start
  206.9 44.6 %adamw.3 = (bf16[16,96,2304]{2,1,0:T(8,128)(2,1)}, bf16[16,96,2304]{2,1,0:T(8,128)(2,1)}, bf16[2,9,8,32,768]{4,3,2,1,0:T(8,128)(2,1)}, f32[16,96,2304]{2,1,0:T(8...) custom-call(f32[8,128]{1,0:T(8,128)} %get-tuple-element.82.f_ref, ...), custom_call_target="tpu_custom_call" | custom-call | flops 119439360 | bytes 131383296 | tf_op jit(solution)/shard_map/adamw/pallas_call | solution.py:381
  251.5 0.0 collective-permute-done.3.refs_0_
  251.5 0.0 collective-permute-done.2.refs_3_
  251.5 0.0 collective-permute-done.1.refs_2_
  251.6 0.0 collective-permute-done.refs_1_
  251.6 0.1 collective-permute-start.4
  251.7 0.5 collective-permute-start.5
  252.2 0.1 collective-permute-start.6
  252.3 21.1 %adamw.4 = (bf16[16,96,2304]{2,1,0:T(8,128)(2,1)}, bf16[16,96,2304]{2,1,0:T(8,128)(2,1)}, bf16[2,9,8,32,768]{4,3,2,1,0:T(8,128)(2,1)}, f32[16,96,2304]{2,1,0:T(8...) custom-call(f32[8,128]{1,0:T(8,128)} %get-tuple-element.82.f_ref, ...), custom_call_target="tpu_custom_call", output_to_operand_aliasing={{0}: (14, {}), {1}: (15, {}), {2}: (16, {}), {3}: (17, {}),... | custom-call | flops 53084160 | bytes 58392576 | tf_op jit(solution)/shard_map/adamw/pallas_call | solution.py:381
  273.4 0.0 collective-permute-done.4.refs_0_
  273.4 0.0 collective-permute-done.5.refs_1_
  273.4 0.0 collective-permute-done.6.refs_2_
  273.4 15.6 %adamw.5 = (bf16[16,96,2304]{2,1,0:T(8,128)(2,1)}, bf16[16,96,2304]{2,1,0:T(8,128)(2,1)}, bf16[2,9,8,32,768]{4,3,2,1,0:T(8,128)(2,1)}, f32[16,96,2304]{2,1,0:T(8...) custom-call(f32[8,128]{1,0:T(8,128)} %get-tuple-element.82.f_ref, ...), custom_call_target="tpu_custom_call", output_to_operand_aliasing={{0}: (13, {}), {1}: (14, {}), {2}: (15, {}), {3}: (16, {}),... | custom-call | flops 39813120 | bytes 43794432 | tf_op jit(solution)/shard_map/adamw/pallas_call | solution.py:381
Async XLA Ops:
  203.6 47.9 %collective-permute-start.3 = (bf16[9,4,144,128]{3,2,1,0:T(8,128)(2,1)}, bf16[9,4,144,128]{3,2,1,0:T(8,128)(2,1)}, u32[]{:S(2)}, u32[]{:S(2)}) collective-permute-start(bf16[9,4,144,128]{3,2,1,0:T(8,128)(2,1)} %get-tuple-element.83.refs_1_), channel_id=1, source_target_pairs={{0,1},{1,0},{2,3},{3,2},{4,5},{5,4},{6,7},{7,6},{8,9},{9,8},{10,11... | collective-permute-start | bytes 3981320 | tf_op jit(solution)/shard_map/ppermute | solution.py:401
  203.9 47.6 %collective-permute-start.2 = (bf16[9,4,144,128]{3,2,1,0:T(8,128)(2,1)}, bf16[9,4,144,128]{3,2,1,0:T(8,128)(2,1)}, u32[]{:S(2)}, u32[]{:S(2)}) collective-permute-start(bf16[9,4,144,128]{3,2,1,0:T(8,128)(2,1)} %get-tuple-element.83.refs_1_), channel_id=1, source_target_pairs={{0,24},{1,7},{2,26},{3,1},{4,28},{5,3},{6,30},{7,5},{8,0},{9,15},{... | collective-permute-start | bytes 3981320 | tf_op jit(solution)/shard_map/ppermute | solution.py:401
  206.3 45.3 %collective-permute-start.1 = (bf16[9,4,144,128]{3,2,1,0:T(8,128)(2,1)}, bf16[9,4,144,128]{3,2,1,0:T(8,128)(2,1)}, u32[]{:S(2)}, u32[]{:S(2)}) collective-permute-start(bf16[9,4,144,128]{3,2,1,0:T(8,128)(2,1)} %get-tuple-element.83.refs_1_), channel_id=1, source_target_pairs={{0,16},{1,5},{2,18},{3,7},{4,20},{5,1},{6,22},{7,3},{8,24},{9,13},... | collective-permute-start | bytes 3981320 | tf_op jit(solution)/shard_map/ppermute | solution.py:401
  206.3 45.3 %collective-permute-start = (bf16[9,4,144,128]{3,2,1,0:T(8,128)(2,1)}, bf16[9,4,144,128]{3,2,1,0:T(8,128)(2,1)}, u32[]{:S(2)}, u32[]{:S(2)}) collective-permute-start(bf16[9,4,144,128]{3,2,1,0:T(8,128)(2,1)} %get-tuple-element.83.refs_1_), channel_id=1, source_target_pairs={{0,8},{1,3},{2,10},{3,5},{4,12},{5,7},{6,14},{7,1},{8,16},{9,11},{... | collective-permute-start | bytes 3981320 | tf_op jit(solution)/shard_map/ppermute | solution.py:401
  251.6 21.8 %collective-permute-start.4 = (bf16[9,4,144,128]{3,2,1,0:T(8,128)(2,1)}, bf16[9,4,144,128]{3,2,1,0:T(8,128)(2,1)}, u32[]{:S(2)}, u32[]{:S(2)}) collective-permute-start(bf16[9,4,144,128]{3,2,1,0:T(8,128)(2,1)} %collective-permute-done.refs_1_), channel_id=1, source_target_pairs={{0,1},{1,0},{2,3},{3,2},{4,5},{5,4},{6,7},{7,6},{8,9},{9,8},{10,11... | collective-permute-start | bytes 3981320 | tf_op jit(solution)/shard_map/ppermute | solution.py:401
  251.7 21.7 %collective-permute-start.5 = (bf16[9,4,144,128]{3,2,1,0:T(8,128)(2,1)}, bf16[9,4,144,128]{3,2,1,0:T(8,128)(2,1)}, u32[]{:S(2)}, u32[]{:S(2)}) collective-permute-start(bf16[9,4,144,128]{3,2,1,0:T(8,128)(2,1)} %collective-permute-done.1.refs_2_), channel_id=1, source_target_pairs={{0,1},{1,0},{2,3},{3,2},{4,5},{5,4},{6,7},{7,6},{8,9},{9,8},{10,11... | collective-permute-start | bytes 3981320 | tf_op jit(solution)/shard_map/ppermute | solution.py:401
  252.2 21.2 %collective-permute-start.6 = (bf16[9,4,144,128]{3,2,1,0:T(8,128)(2,1)}, bf16[9,4,144,128]{3,2,1,0:T(8,128)(2,1)}, u32[]{:S(2)}, u32[]{:S(2)}) collective-permute-start(bf16[9,4,144,128]{3,2,1,0:T(8,128)(2,1)} %collective-permute-done.2.refs_3_), channel_id=1, source_target_pairs={{0,1},{1,0},{2,3},{3,2},{4,5},{5,4},{6,7},{7,6},{8,9},{9,8},{10,11... | collective-permute-start | bytes 3981320 | tf_op jit(solution)/shard_map/ppermute | solution.py:401
